TPU v7x, 128 devices: a whole 4x4x4 slice. The times are simulated.
128 devices in a mesh: rep: 1, dp: 128 (over x, y, z, core).
Axes of the slice: x: 4, y: 4, z: 4, core: 2. Of those that a mesh axis runs over, the one named last changes fastest.
Arguments:
- x: bfloat16 [128, 1024, 768], P(('rep', 'dp'))
- dy: bfloat16 [128, 1024, 768], P(('rep', 'dp'))
- w_gate: bfloat16 [2, 768, 6144], replicated
- w_up: bfloat16 [2, 768, 6144], replicated
- w_down: bfloat16 [2, 6144, 768], replicated
- m_w_gate: float32 [2, 768, 6144], P(None, 'dp')
- m_w_up: float32 [2, 768, 6144], P(None, 'dp')
- m_w_down: float32 [2, 6144, 768], P(None, 'dp')
- v_w_gate: float32 [2, 768, 6144], P(None, 'dp')
- v_w_up: float32 [2, 768, 6144], P(None, 'dp')
- v_w_down: float32 [2, 6144, 768], P(None, 'dp')
Outputs:
- output 1: bfloat16 [2, 768, 6144], P('rep')
- output 2: bfloat16 [2, 768, 6144], P('rep')
- output 3: bfloat16 [2, 6144, 768], P('rep')
- output 4: float32 [2, 768, 6144], P('rep', 'dp')
- output 5: float32 [2, 768, 6144], P('rep', 'dp')
- output 6: float32 [2, 6144, 768], P('rep', 'dp')
- output 7: float32 [2, 768, 6144], P('rep', 'dp')
- output 8: float32 [2, 768, 6144], P('rep', 'dp')
- output 9: float32 [2, 6144, 768], P('rep', 'dp')
All inputs are finite; a program needn't handle non-finite values.
Results may differ from a plain program's by a relative error of at most 0.022.
Values are sent between devices in bfloat16 or wider.
A program may use at most 1.5 GiB of HBM per device.

v0:
```python
import jax
import jax.numpy as jnp
from jax import lax

NAMES = ("w_gate", "w_up", "w_down")


def matmul(a, w):
    return jnp.dot(a, w, preferred_element_type=jnp.float32).astype(jnp.bfloat16)


def normed(h):
    wide = h.astype(jnp.float32)
    scale = lax.rsqrt(jnp.mean(wide**2, -1, keepdims=True) + 1e-6)
    return (wide * scale).astype(jnp.bfloat16)


def layer(h, w):
    a = normed(h)
    gate = jnp.dot(a, w["w_gate"], preferred_element_type=jnp.float32)
    up = jnp.dot(a, w["w_up"], preferred_element_type=jnp.float32)
    return h + matmul((jax.nn.silu(gate) * up).astype(jnp.bfloat16), w["w_down"])


def adamw(w, m, v, g):
    m = 0.9 * m + 0.1 * g
    v = 0.95 * v + 0.05 * g * g
    step = m * lax.rsqrt(v + 1e-8) + 0.1 * w
    return (w - 0.02 * step).astype(jnp.bfloat16), m, v


def clipped(gradients, sum_of_squares, count):
    factor = jnp.minimum(1.0, 0.5 * lax.rsqrt(sum_of_squares / count + 1e-30))
    return [g * factor for g in gradients]


def stack(weights, h):
    for number in range(weights["w_gate"].shape[0]):
        h = layer(h, {name: w[number] for name, w in weights.items()})
    return h


def solution(mesh):
    groups = mesh.shape["rep"]

    def step(x, dy, *arrays):
        weights, m, v = (arrays[i : i + 3] for i in (0, 3, 6))
        x, dy = (t.reshape(groups, -1, *t.shape[1:]) for t in (x, dy))

        def of_a_group(x, dy):
            _, back = jax.vjp(lambda w: stack(w, x), dict(zip(NAMES, weights, strict=True)))
            by_weights = back(dy)[0]
            gradients = [by_weights[name].astype(jnp.float32) for name in NAMES]
            gradients = clipped(gradients, sum(jnp.sum(g * g) for g in gradients), sum(g.size for g in gradients))
            new = [adamw(w.astype(jnp.float32), m, v, g) for w, m, v, g in zip(weights, m, v, gradients, strict=True)]
            return tuple(one[which] for which in range(3) for one in new)

        return tuple(t.reshape(-1, *t.shape[2:]) for t in jax.vmap(of_a_group)(x, dy))

    return step
```

profile of v0, /device:TPU:1, one launch (start us, length us, event | category | flops | bytes accessed | tf_op | source)
XLA Modules:
  0.0 2278.0 jit_solution(6522347292043234920)
XLA Ops:
  10.8 19.1 fusion.51
  29.9 17.2 fusion.49
  47.1 21.2 fusion.30
  84.3 17.5 fusion.41
  101.8 17.1 fusion.44
  136.6 21.0 fusion.10
  175.3 21.8 fusion.69
  251.0 29.2 %fusion.14 = f32[6144,768]{0,1:T(8,128)} fusion(f32[1024,6144]{1,0:T(8,128)} %fusion.51, f32[1024,6144]{1,0:T(8,128)} %fusion.49, bf16[1024,6144]{1,0:T(8,128)(2,1)} %convolution_convert_fusion, bf16[1,1024,768]{2,1,0:T(8,128)(2,1)S(1)} %copy-done.4, f32[1024]{0:T(1024)S(1)} %copy-done.65), kind=kOutput, calls=%fused_computation.15 | convolution fusion | flops 9735241728 | bytes 83365888 | tf_op jit(solution)/vmap(transpose(jvp()))/dot_general | solution.py:20
  280.2 432.9 %fusion.145 = (f32[6144,8]{0,1:T(8,128)S(1)}, f32[6144,8]{0,1:T(8,128)S(1)}) fusion(f32[6144,768]{0,1:T(8,128)} %fusion.14, f32[6144,768]{0,1:T(8,128)} %fusion.95), kind=kCustom, calls=%all-reduce-scatter.4 | all-reduce-scatter fusion | flops 12582913 | bytes 38141952
  718.3 28.3 %fusion.32 = f32[6144,768]{1,0:T(8,128)} fusion(f32[1024,6144]{1,0:T(8,128)} %fusion.44, f32[1024,6144]{1,0:T(8,128)} %fusion.41, bf16[1,1024,768]{2,1,0:T(8,128)(2,1)} %param.2), kind=kOutput, calls=%fused_computation.37 | convolution fusion | flops 9701425152 | bytes 70778880 | tf_op jit(solution)/vmap(transpose(jvp()))/dot_general | solution.py:9
  748.1 23.7 %fusion.26 = f32[6144,768]{0,1:T(8,128)} fusion(bf16[1024,6144]{1,0:T(8,128)(2,1)} %convolution_convert_fusion.1, f32[1024,6144]{1,0:T(8,128)} %fusion.41, bf16[1,1024,768]{1,2,0:T(8,128)(2,1)S(1)} %copy-done.1, f32[1024]{0:T(1024)S(1)} %bitcast.335), kind=kOutput, calls=%fused_computation.33 | convolution fusion | flops 9703784448 | bytes 58200064 | tf_op jit(solution)/vmap(transpose(jvp()))/dot_general | solution.py:21
  771.8 23.9 %fusion.6 = f32[6144,768]{0,1:T(8,128)} fusion(bf16[1024,6144]{1,0:T(8,128)(2,1)} %convolution_convert_fusion, f32[1024,6144]{1,0:T(8,128)} %fusion.51, bf16[1,1024,768]{2,1,0:T(8,128)(2,1)S(1)} %copy-done.4, f32[1024]{0:T(1024)S(1)} %copy-done.65), kind=kOutput, calls=%fused_computation.8 | convolution fusion | flops 9703784448 | bytes 58200064 | tf_op jit(solution)/vmap(transpose(jvp()))/dot_general | solution.py:21
  795.6 435.1 %fusion.146 = (f32[6144,8]{0,1:T(8,128)S(1)}, f32[6144,8]{0,1:T(8,128)S(1)}) fusion(f32[6144,768]{0,1:T(8,128)} %fusion.6, f32[6144,768]{0,1:T(8,128)} %fusion.26), kind=kCustom, calls=%all-reduce-scatter.5 | all-reduce-scatter fusion | flops 12582913 | bytes 38141952
  1249.1 18.2 collective-permute-start.54
  1576.4 59.6 %concatenate.1 = bf16[6144,262]{0,1:T(8,128)(2,1)S(1)} concatenate(bf16[6144,6]{0,1:T(8,128)(2,1)} %collective-permute-done.63, bf16[6144,8]{0,1:T(8,128)(2,1)} %copy-done.16, bf16[6144,8]{0,1:T(8,128)(2,1)} %copy-done.17, bf16[6144,8]{0,1:T(8,128)(2,1)} %copy-done.18, bf16[6144,8]{0,1:T(8,128)(2,1)} %copy-done.19, bf16[6144,8]{0,1:T(8,128)(2,1)} %copy-done.20, ...), dimensions={1} | concatenate | bytes 6537216
  1636.0 97.7 %concatenate = bf16[6144,262]{0,1:T(8,128)(2,1)} concatenate(bf16[6144,6]{0,1:T(8,128)(2,1)} %collective-permute-done.31, bf16[6144,8]{0,1:T(8,128)(2,1)} %copy-done.47, bf16[6144,8]{0,1:T(8,128)(2,1)} %copy-done.48, bf16[6144,8]{0,1:T(8,128)(2,1)} %copy-done.49, bf16[6144,8]{0,1:T(8,128)(2,1)} %copy-done.50, bf16[6144,8]{0,1:T(8,128)(2,1)} %copy-done.51, ...), dimensions={1} | concatenate | bytes 6537216
  1733.7 97.7 %concatenate.3 = bf16[6144,262]{0,1:T(8,128)(2,1)} concatenate(bf16[6144,6]{0,1:T(8,128)(2,1)} %copy-done.15, bf16[6144,8]{0,1:T(8,128)(2,1)} %collective-permute-done.126, bf16[6144,8]{0,1:T(8,128)(2,1)} %collective-permute-done.125, bf16[6144,8]{0,1:T(8,128)(2,1)} %collective-permute-done.124, bf16[6144,8]{0,1:T(8,128)(2,1)} %collective-permute-done.123, ...), dimensions={1} | concatenate | bytes 6537216
  1831.4 97.2 %concatenate.2 = bf16[6144,262]{0,1:T(8,128)(2,1)} concatenate(bf16[6144,6]{0,1:T(8,128)(2,1)} %copy-done.14, bf16[6144,8]{0,1:T(8,128)(2,1)} %collective-permute-done.94, bf16[6144,8]{0,1:T(8,128)(2,1)} %collective-permute-done.93, bf16[6144,8]{0,1:T(8,128)(2,1)} %collective-permute-done.92, bf16[6144,8]{0,1:T(8,128)(2,1)} %collective-permute-done.91, ...), dimensions={1} | concatenate | bytes 6537216
  1936.9 62.7 %all-reduce.10 = f32[]{:T(128)} all-reduce(f32[]{:T(128)S(6)} %add.102), channel_id=3, replica_groups=mesh['rep'=1,'dp'=128] {'dp'}, use_global_device_ids=true, to_apply=%region_3.4.clone | all-reduce | flops 1 | bytes 8 | tf_op jit(solution)/vmap()/reduce_sum | solution.py:54
  2011.3 72.1 %all-gather.10.cloned.1.call-done = bf16[1,2,768,6144]{3,1,0,2:T(2,128)(2,1)} async-done(((bf16[1,2,6,6144]{3,1,0,2:T(2,128)(2,1)}), bf16[1,2,768,6144]{3,1,0,2:T(2,128)(2,1)}) %all-gather.10.cloned.1.call-update) | async-done | bytes 18874384 | tf_op jit(solution)/reshape | solution.py:58
  2083.4 20.4 copy.18
  2103.8 65.5 %all-gather.12.cloned.1.call-done = bf16[1,2,768,6144]{3,1,0,2:T(2,128)(2,1)} async-done(((bf16[1,2,6,6144]{3,1,0,2:T(2,128)(2,1)}), bf16[1,2,768,6144]{3,1,0,2:T(2,128)(2,1)}) %all-gather.12.cloned.1.call-update) | async-done | bytes 18874384 | tf_op jit(solution)/reshape | solution.py:58
  2169.3 20.4 copy.19
  2189.7 64.9 %all-gather.14.cloned.1.call-done = bf16[1,2,6144,768]{3,2,1,0:T(8,128)(2,1)} async-done(((bf16[1,2,48,768]{3,2,1,0:T(8,128)(2,1)}), bf16[1,2,6144,768]{3,2,1,0:T(8,128)(2,1)}) %all-gather.14.cloned.1.call-update) | async-done | bytes 18874384 | tf_op jit(solution)/reshape | solution.py:58
  (439 shorter events, 475.0 us)
Async XLA Ops:
  7.2 1926.5 %reduce-scatter.21.cloned.1.call-start = ((), (), s32[]{:S(2)}) async-start(), calls=%async_computation.6 | async-start | bytes 19021824
  217.8 1716.8 %reduce-scatter.19.cloned.1.call-start = ((), (), s32[]{:S(2)}) async-start(), calls=%async_computation.5 | async-start | bytes 19021824
  713.8 521.0 %collective-permute-start.63 = (bf16[6144,6]{0,1:T(8,128)(2,1)}, bf16[6144,6]{0,1:T(8,128)(2,1)}, u32[]{:S(2)}, u32[]{:S(2)}) collective-permute-start(bf16[6144,6]{0,1:T(8,128)(2,1)} %slice.25), channel_id=1, source_target_pairs={{0,32},{1,33},{2,34},{3,35},{4,36},{5,37},{6,38},{7,39},{8,40},{9,... | collective-permute-start | bytes 221192
  716.4 519.7 %collective-permute-start.31 = (bf16[6144,6]{0,1:T(8,128)(2,1)}, bf16[6144,6]{0,1:T(8,128)(2,1)}, u32[]{:S(2)}, u32[]{:S(2)}) collective-permute-start(bf16[6144,6]{0,1:T(8,128)(2,1)} %slice.24), channel_id=1, source_target_pairs={{0,32},{1,33},{2,34},{3,35},{4,36},{5,37},{6,38},{7,39},{8,40},{9,... | collective-permute-start | bytes 221192
  746.7 1336.7 %all-gather.10.cloned.1.call-start = ((), (), s32[]{:S(2)}) async-start(), calls=%async_computation.2 | async-start | bytes 19021824 | tf_op jit(solution)/reshape | solution.py:58
  1243.9 23.5 %collective-permute-start.58 = (bf16[6144,8]{0,1:T(8,128)(2,1)S(1)}, bf16[6144,8]{0,1:T(8,128)(2,1)S(1)}, u32[]{:S(2)}, u32[]{:S(2)}) collective-permute-start(bf16[6144,8]{0,1:T(8,128)(2,1)S(1)} %convert.290), channel_id=1, source_target_pairs={{0,27},{1,28},{2,29},{3,30},{4,31},{5,32},{6,33},{7,34},{8,35},{9,... | collective-permute-start | bytes 294920
  1245.2 25.7 %collective-permute-start.57 = (bf16[6144,8]{0,1:T(8,128)(2,1)S(1)}, bf16[6144,8]{0,1:T(8,128)(2,1)S(1)}, u32[]{:S(2)}, u32[]{:S(2)}) collective-permute-start(bf16[6144,8]{0,1:T(8,128)(2,1)S(1)} %convert.290), channel_id=1, source_target_pairs={{0,26},{1,27},{2,28},{3,29},{4,30},{5,31},{6,32},{7,33},{8,34},{9,... | collective-permute-start | bytes 294920
  1246.5 27.3 %collective-permute-start.56 = (bf16[6144,8]{0,1:T(8,128)(2,1)S(1)}, bf16[6144,8]{0,1:T(8,128)(2,1)S(1)}, u32[]{:S(2)}, u32[]{:S(2)}) collective-permute-start(bf16[6144,8]{0,1:T(8,128)(2,1)S(1)} %convert.290), channel_id=1, source_target_pairs={{0,25},{1,26},{2,27},{3,28},{4,29},{5,30},{6,31},{7,32},{8,33},{9,... | collective-permute-start | bytes 294920
  1247.8 28.3 %collective-permute-start.55 = (bf16[6144,8]{0,1:T(8,128)(2,1)S(1)}, bf16[6144,8]{0,1:T(8,128)(2,1)S(1)}, u32[]{:S(2)}, u32[]{:S(2)}) collective-permute-start(bf16[6144,8]{0,1:T(8,128)(2,1)S(1)} %convert.290), channel_id=1, source_target_pairs={{0,24},{1,25},{2,26},{3,27},{4,28},{5,29},{6,30},{7,31},{8,32},{9,... | collective-permute-start | bytes 294920
  1249.1 29.3 %collective-permute-start.54 = (bf16[6144,8]{0,1:T(8,128)(2,1)S(1)}, bf16[6144,8]{0,1:T(8,128)(2,1)S(1)}, u32[]{:S(2)}, u32[]{:S(2)}) collective-permute-start(bf16[6144,8]{0,1:T(8,128)(2,1)S(1)} %convert.290), channel_id=1, source_target_pairs={{0,23},{1,24},{2,25},{3,26},{4,27},{5,28},{6,29},{7,30},{8,31},{9,... | collective-permute-start | bytes 294920
  1371.2 18.5 collective-permute-start.14
  1373.4 18.3 collective-permute-start.13
  1452.1 18.9 collective-permute-start.110
  1454.1 18.9 collective-permute-start.109
  1532.5 19.4 collective-permute-start.78
  1534.5 19.4 collective-permute-start.77
  1538.3 17.5 collective-permute-start.76
  1562.1 269.3 %collective-permute-start.68 = (bf16[6144,8]{0,1:T(8,128)(2,1)S(1)}, bf16[6144,8]{0,1:T(8,128)(2,1)}, u32[]{:S(2)}, u32[]{:S(2)}) collective-permute-start(bf16[6144,8]{0,1:T(8,128)(2,1)S(1)} %convert.287), channel_id=1, source_target_pairs={{0,5},{1,6},{2,7},{3,8},{4,9},{5,10},{6,11},{7,12},{8,13},{9,14},{... | collective-permute-start | bytes 294920
  1564.5 266.9 %collective-permute-start.67 = (bf16[6144,8]{0,1:T(8,128)(2,1)S(1)}, bf16[6144,8]{0,1:T(8,128)(2,1)}, u32[]{:S(2)}, u32[]{:S(2)}) collective-permute-start(bf16[6144,8]{0,1:T(8,128)(2,1)S(1)} %convert.287), channel_id=1, source_target_pairs={{0,4},{1,5},{2,6},{3,7},{4,8},{5,9},{6,10},{7,11},{8,12},{9,13},{1... | collective-permute-start | bytes 294920
  1567.2 264.2 %collective-permute-start.66 = (bf16[6144,8]{0,1:T(8,128)(2,1)S(1)}, bf16[6144,8]{0,1:T(8,128)(2,1)}, u32[]{:S(2)}, u32[]{:S(2)}) collective-permute-start(bf16[6144,8]{0,1:T(8,128)(2,1)S(1)} %convert.287), channel_id=1, source_target_pairs={{0,3},{1,4},{2,5},{3,6},{4,7},{5,8},{6,9},{7,10},{8,11},{9,12},{10... | collective-permute-start | bytes 294920
  1571.1 260.4 %collective-permute-start.65 = (bf16[6144,8]{0,1:T(8,128)(2,1)S(1)}, bf16[6144,8]{0,1:T(8,128)(2,1)}, u32[]{:S(2)}, u32[]{:S(2)}) collective-permute-start(bf16[6144,8]{0,1:T(8,128)(2,1)S(1)} %convert.287), channel_id=1, source_target_pairs={{0,2},{1,3},{2,4},{3,5},{4,6},{5,7},{6,8},{7,9},{8,10},{9,11},{10,... | collective-permute-start | bytes 294920
  1573.1 258.3 %collective-permute-start.64 = (bf16[6144,8]{0,1:T(8,128)(2,1)S(1)}, bf16[6144,8]{0,1:T(8,128)(2,1)}, u32[]{:S(2)}, u32[]{:S(2)}) collective-permute-start(bf16[6144,8]{0,1:T(8,128)(2,1)S(1)} %convert.287), channel_id=1, source_target_pairs={{0,1},{1,2},{2,3},{3,4},{4,5},{5,6},{6,7},{7,8},{8,9},{9,10},{10,1... | collective-permute-start | bytes 294920
  2002.8 166.5 %all-gather.12.cloned.1.call-start = ((), (), s32[]{:S(2)}) async-start(), calls=%async_computation.3 | async-start | bytes 19021824 | tf_op jit(solution)/reshape | solution.py:58
  2005.3 249.3 %all-gather.14.cloned.1.call-start = ((), (), s32[]{:S(2)}) async-start(), calls=%async_computation.4 | async-start | bytes 19021824 | tf_op jit(solution)/reshape | solution.py:58
  (175 other events, 13394.8 us)
Sparse Core Ops, SparseCore 0:
  217.9 266.9 reduce-scatter.20
  746.8 257.7 reduce-scatter.18
  2002.9 80.4 all-gather.9
  2086.8 82.3 all-gather.11
  2172.2 82.3 all-gather.13
where the time goes:
time: 2310 us; the launch traced here: 2280 us
  blocking collectives  931 us (40%)
  local copies, waits for them, and re-layouts  430 us (19%)
  starting transfers between devices  346 us (15%)
  matrix products  293 us (13%)
  waiting for transfers between devices  205 us (9%)
  other arithmetic  55.4 us (2%)
    unnamed x2, blocking collectives  868 us
    unnamed x149, local copies, waits for them, and re-layouts  426 us
    unnamed x130, starting transfers between devices  346 us
    reshape x3, waiting for transfers between devices, step(): t.reshape(-1, *t.shape[2:])  203 us
    dot_general x5, matrix products, layer(): up = jnp.dot(a, w['w_up'], preferred_element_type=jnp.float32)  104 us
    dot_general x5, matrix products, layer(): gate = jnp.dot(a, w['w_gate'], preferred_element_type=jnp.float32)  95.7 us
    dot_general x5, matrix products, matmul(): jnp.dot(a, w, preferred_element_type=jnp.float32).astype(jnp.bfloat16)  93.5 us
    reduce_sum x1, blocking collectives, of_a_group(): jnp.sum(g * g)  62.7 us
  transfers between devices with their start and end apart: 133, of which 4 were waited for; matrix products, arithmetic and copies ran while one was open for 62% of the time, Pallas kernels for 0%

commit v1 on v0

v1 whole, which is shorter than its diff:
```python
import functools

import jax
import jax.numpy as jnp
from jax import lax
from jax.experimental import pallas as pl
from jax.experimental.pallas import tpu as pltpu
from jax.sharding import PartitionSpec as P

F32, BF16 = jnp.float32, jnp.bfloat16
MESH = pl.DeviceIdType.MESH
ALL = slice(None)
VMEM = pl.BlockSpec(memory_space=pltpu.VMEM)
ANY = pl.BlockSpec(memory_space=pl.ANY)
PARAMS = pltpu.CompilerParams
DMA = pltpu.SemaphoreType.DMA
SIGNALS = pltpu.SemaphoreType.REGULAR

RING, CORES, LAYERS = 4, 2, 2
TORUS = (RING, RING, RING)
AXES = range(len(TORUS))
PARTS = len(TORUS)
PAIR = range(2)
GROUP = RING * CORES
PLANE = RING * RING
OWN = 6
ROWS = OWN * GROUP
HALF = 128
LANES = 2 * HALF
T, D, FF = 1024, 768, 6144
NB = 512
N_J = FF // NB
STRIP = 256


def mib(n):
    return n << 20


def begin(copies):
    for c in copies:
        c.start()


def end(copies):
    for c in copies:
        c.wait()


def received(copies):
    for c in copies:
        c.wait_recv()


def sent(copies):
    for c in copies:
        c.wait_send()


def loop(n, first=0):
    def run(body):
        lax.fori_loop(first, n, lambda i, _: body(i), None)

    return run


def slot(i):
    return i % len(PAIR)


def columns(j, n=NB):
    return pl.ds(pl.multiple_of(j * n, n), n)


def lanes(q, n=HALF):
    return pl.ds(q * n, n)


def around(q):
    return q % RING


def place():
    p = lax.axis_index("dp")
    q = p // CORES
    return (q // PLANE, around(q // RING), around(q)), p % CORES


def number(coords, core):
    x, y, z = coords
    return ((x * RING + y) * RING + z) * CORES + core


def device(coords, core):
    return {"dp": number(coords, core)}


def moved(coords, axis, by):
    return tuple(around(q + by) if a == axis else q for a, q in enumerate(coords))


def signal(sem, where):
    pl.semaphore_signal(sem, inc=1, device_id=where, device_id_type=MESH)


def remote(src, dst, send, recv, where):
    return pltpu.make_async_remote_copy(src_ref=src, dst_ref=dst, send_sem=send, recv_sem=recv, device_id=where, device_id_type=MESH)


def group_peers(coords, core):
    x, y, z = coords
    return [((x, y, around(z + dz)), (core + dc) % CORES) for dz in range(RING) for dc in range(CORES) if dz or dc]


def plane_peers(coords, core):
    x, y, z = coords
    return [((around(x + dx), around(y + dy), z), core) for dx in range(RING) for dy in range(RING) if dx or dy]


def enter(coords, core):
    barrier = pltpu.get_barrier_semaphore()
    peers = group_peers(coords, core) + plane_peers(coords, core)
    for where, c in peers:
        signal(barrier, device(where, c))
    pl.semaphore_wait(barrier, len(peers))


GATE, UP, DOWN = range(3)
ORDER = [(1, which, half) for half in PAIR for which in (GATE, UP)]
ORDER += [(layer, DOWN, half) for layer in (1, 0) for half in PAIR]
ORDER += [(0, which, half) for half in PAIR for which in (GATE, UP)]
UNITS = len(ORDER)
UNIT = {what: u for u, what in enumerate(ORDER)}
WIDE1, DOWN1, DOWN0, WIDE0 = UNIT[1, GATE, 0], UNIT[1, DOWN, 0], UNIT[0, DOWN, 0], UNIT[0, GATE, 0]
EACH = UNITS // LAYERS
AHEAD = len(PAIR)
SIDES = ((0, 1), (1, -1))
PASSED, DIRECT = 1, 0
CELL = (ROWS, HALF)


def tile(half):
    return pl.ds(16 * half, 16 + 16 * half)


def pair_of(half):
    return pl.ds(2 * half, 2)


class Ring:
    def __init__(self, k, stage, coords, core, bufs, ss, rs, credit):
        self.axes = axes_left(k, stage)
        self.axis, self.cut = (k + stage) % PARTS, (k - 1) % PARTS
        self.last = self.axis == self.cut
        self.coords, self.core = coords, core
        self.data, self.ra, self.rb = bufs
        self.ss, self.rs, self.credit = ss, rs, credit
        self.i = coords[self.axis]

    def to(self, by):
        return device(moved(self.coords, self.axis, by), self.core)

    def index(self, place, half):
        at = [place if a == self.axis else pair_of(half) if a == self.cut else ALL for a in self.axes]
        return (*at, tile(half) if self.last else ALL, ALL)

    def landing(self, half):
        return (tile(half), ALL) if self.last else ()

    def out(self, half):
        return self.landing(half) or (*(pair_of(half) if a == self.cut else ALL for a in self.axes if a != self.axis), ALL, ALL)

    def firsts(self):
        out = {}
        for side, by in SIDES:
            for which, step, half in ((PASSED, by + by, 1 - side), (DIRECT, by, side)):
                at = self.index(around(self.i + step), half)
                n = len(out)
                out[side, which] = remote(self.data.at[at], self.ra.at[(side, which) + self.landing(half)], self.ss.at[n], self.rs.at[n], self.to(by))
        return out

    def seconds(self):
        out = []
        for side, by in SIDES:
            at, n = self.landing(1 - side), len(SIDES) * len(PAIR) + side
            out.append(remote(self.ra.at[(side, PASSED) + at], self.rb.at[(side,) + at], self.ss.at[n], self.rs.at[n], self.to(by)))
        return out

    def start(self, again):
        @pl.when(again)
        def _():
            for side, _by in SIDES:
                pl.semaphore_wait(self.credit.at[side], 1)

        begin(self.firsts().values())

    def middle(self):
        copies = self.firsts()
        for side, by in SIDES:
            half = 1 - side
            at = (side, PASSED) + self.landing(half)
            copies[side, PASSED].wait_recv()
            here = self.data[self.index(around(self.i + by), half)].astype(F32)
            self.ra[at] = (here + self.ra[at].astype(F32)).astype(BF16)
        begin(self.seconds())

    def finish(self, store, more):
        copies, passed = self.firsts(), self.seconds()
        for side, _by in SIDES:
            copies[side, DIRECT].wait_recv()
            passed[side].wait_recv()
        for half in PAIR:
            here = self.data[self.index(self.i, half)].astype(F32)
            near = self.ra[(half, DIRECT) + self.landing(half)].astype(F32)
            far = self.rb[(1 - half,) + self.landing(half)].astype(F32)
            store(self.out(half), here + near + far)
        sent([*copies.values(), *passed])

        @pl.when(more)
        def _():
            for side, by in SIDES:
                signal(self.credit.at[side], self.to(-by))


def axes_left(k, stage):
    done = [(k + s) % PARTS for s in range(stage)]
    return [a for a in AXES if a not in done]


class Scatter:
    def __init__(self, grads, bufs, sems):
        self.grads = grads
        self.coords, self.core = place()
        self.partner = device(self.coords, 1 - self.core)
        self.d1, self.r0, self.stages, self.blocks, self.squares = bufs
        self.load_sem, self.s_send, self.s_recv, self.ssem, self.rsem, self.credit, self.s_credit = sems

    def load(self, u, k, layer=0):
        src = self.grads[layer].at[u % EACH, k, self.core]
        return pltpu.make_async_copy(src, self.d1.at[slot(u), k], self.load_sem.at[slot(u), k])

    def swap(self, u, k, layer=0):
        s = slot(u)
        src = self.grads[layer].at[u % EACH, k, 1 - self.core]
        return remote(src, self.r0.at[s, k], self.s_send.at[s, k], self.s_recv.at[s, k], self.partner)

    def rings(self, u, stage):
        s = slot(u)
        return [
            Ring(k, stage, self.coords, self.core, [b.at[s] for b in self.stages[stage][k]], self.ssem.at[s, k, stage], self.rsem.at[s, k, stage],
                 self.credit.at[k, stage])
            for k in range(PARTS)
        ]

    def feed(self, u):
        @pl.when(u >= AHEAD)
        def _():
            pl.semaphore_wait(self.s_credit, 1)

        for layer, its in ((1, u < EACH), (0, u >= EACH)):

            @pl.when(its)
            def _(layer=layer):
                for k in range(PARTS):
                    begin([self.swap(u, k, layer), self.load(u, k, layer)])

    def add(self, u):
        for k in range(PARTS):
            self.load(u, k).wait()
            self.swap(u, k).wait_recv()
            d1, r0 = self.d1.at[slot(u), k], self.r0.at[slot(u), k]

            @loop(PLANE)
            def _(n, d1=d1, r0=r0):
                at = (n // RING, around(n))
                d1[at] = (d1[at].astype(F32) + r0[at].astype(F32)).astype(BF16)

        sent([self.swap(u, k) for k in range(PARTS)])

        @pl.when(u + AHEAD < UNITS)
        def _():
            signal(self.s_credit, self.partner)

        for ring in self.rings(u, 0):
            ring.start(u >= AHEAD)

    def at_stages(self, i, step):
        for stage in AXES:
            u = i - stage

            @pl.when((u >= 0) & (u < UNITS))
            def _(u=u, stage=stage):
                step(u, stage)

    def middles(self, i):
        def step(u, stage):
            for ring in self.rings(u, stage):
                ring.middle()

        self.at_stages(i, step)

    def finishes(self, i):
        def step(u, stage):
            rings = self.rings(u, stage)
            for k, ring in enumerate(rings):
                ring.finish(self.into(u, k, ring, stage), u + AHEAD < UNITS)
            if not rings[0].last:
                for ring in self.rings(u, stage + 1):
                    ring.start(u >= AHEAD)

        self.at_stages(i, step)

    def into(self, u, k, ring, stage):
        def store(at, value):
            value = value.astype(BF16)
            if not ring.last:
                self.stages[stage + 1][k][0][(slot(u),) + at] = value
                return
            self.blocks[(u, k) + at] = value
            value = value.astype(F32)
            self.squares[:] += jnp.sum((value * value).reshape(-1, *self.squares.shape), axis=0)

        return store


PACKED = 80


def packed_row(layer, which, k):
    return OWN * ((layer * len(PAIR) + which) * PARTS + k)


def scatter_scratch():
    two = (len(PAIR),)
    out = [pltpu.VMEM((*two, PARTS, *TORUS, *CELL), BF16)] * len(PAIR)
    for stage in AXES:
        for k in range(PARTS):
            left = [len(PAIR) if a == (k - 1) % PARTS else RING for a in axes_left(k, stage + 1)]
            if left:
                out.append(pltpu.VMEM((*two, *(RING for _ in left), *CELL), BF16))
            out.append(pltpu.VMEM((*two, *two, *two, *left, *CELL), BF16))
            out.append(pltpu.VMEM((*two, *two, *left, *CELL), BF16))
    each = (*two, PARTS)
    out += [pltpu.VMEM((UNITS, PARTS, *CELL), BF16), pltpu.VMEM((8, HALF), F32)]
    out += [DMA(each)] * PARTS + [DMA((*each, PARTS, 6))] * len(PAIR) + [SIGNALS((PARTS, PARTS, *two)), SIGNALS]
    out += [pltpu.VMEM((PACKED, LANES), F32), pltpu.VMEM((GROUP, PACKED, LANES), BF16), pltpu.VMEM((GROUP, PACKED, LANES), BF16)]
    out += [pltpu.VMEM((PLANE, *two, 8, HALF), F32)]
    return out + [DMA((GROUP,))] * 4 + [DMA((PLANE,))] * 2


def scatter_of(grads, scratch):
    scratch = iter(scratch)
    d1, r0 = next(scratch), next(scratch)
    stages = []
    data = [d1.at[:, k] for k in range(PARTS)]
    for stage in AXES:
        row, after = [], []
        for k in range(PARTS):
            if axes_left(k, stage + 1):
                after.append(next(scratch))
            row.append((data[k], next(scratch), next(scratch)))
        stages.append(row)
        data = after
    blocks, squares, *rest = scratch
    return Scatter(grads, (d1, r0, stages, blocks, squares), rest[:7]), rest[7:]


def last_swap(sc, out_ref, own_ref, ss_ref, stage, pack, take, sq, t_send, t_recv, q_send, q_recv, q2_send, q2_recv):
    coords, core = sc.coords, sc.core
    x, y, z = coords
    me = CORES * z + core
    first, second = (sq.at[:, i] for i in PAIR)
    peers = list(enumerate(group_peers(coords, core)))
    first[me] = sc.squares[:]
    squares = [remote(first.at[me], first.at[me], q_send.at[n], q_recv.at[n], device(where, c)) for n, (where, c) in peers]
    takes = [remote(pack.at[CORES * where[-1] + c], take.at[me], t_send.at[n], t_recv.at[n], device(where, c)) for n, (where, c) in peers]
    begin(squares)
    stage[:] = jnp.zeros_like(stage)
    for j in range(GROUP):
        for u, (layer, which, half) in enumerate(ORDER):
            for k in range(PARTS):
                if which != DOWN:
                    stage[pl.ds(packed_row(layer, which, k), OWN), lanes(half)] = sc.blocks[u, k].astype(F32)[OWN * j : OWN * j + OWN]
        pack[j] = stage[:].astype(BF16)
    begin(takes)
    for u, (layer, which, half) in enumerate(ORDER):
        for k in range(PARTS):
            if which == DOWN:
                own_ref[layer, :, lanes(half * PARTS + k)] = sc.blocks[u, k].astype(F32)
    take[me] = pack[me]
    received(squares)
    total = sum(first[j] for j in range(GROUP))
    sent(squares)
    mine = RING * x + y
    second[mine] = total
    squares = [
        remote(second.at[mine], second.at[mine], q2_send.at[n], q2_recv.at[n], device(where, c)) for n, (where, c) in enumerate(plane_peers(coords, core))
    ]
    begin(squares)
    end(takes)
    out_ref[:] = take[:]
    end(squares)
    ss_ref[:] = sum(second[j] for j in range(PLANE))


def gather_kernel(rows_ref, down_ref, wide_out, down0_out, down1_out, last_out, take, stage, t_send, t_recv, own_sem, send, recv, c_send, c_recv):
    coords, core = place()
    x, y, z = coords
    me = CORES * z + core
    partner = device(coords, 1 - core)
    enter(coords, core)
    swaps = []
    for n, (where, c) in enumerate(group_peers(coords, core)):
        swaps.append(remote(rows_ref.at[CORES * where[-1] + c], take.at[me], t_send.at[n], t_recv.at[n], device(where, c)))
    begin(swaps)
    take[me] = rows_ref[me]
    here = (*coords, core)
    own = pltpu.make_async_copy(down_ref.at[1, :, lanes(PARTS - 1, LANES)], last_out.at[here], own_sem)
    own.start()
    down0_out[here] = down_ref[0]
    down1_out[here] = down_ref[1, :, pl.ds(0, D - LANES)]

    def piece(which, k, layer, spot):
        at = tuple(ALL if q is None else q for q in spot)
        if which == DOWN:
            if layer and k == PARTS - 1:
                return last_out.at[(*at, core)]
            return (down0_out, down1_out)[layer].at[(*at, core, ALL, lanes(k, LANES))]
        base = (k * GROUP + core * RING) * LANES
        many = RING if spot[-1] is None else 1
        if many == 1:
            base += spot[-1] * LANES
        return wide_out.at[(layer, which, *at[:-1], ALL, pl.ds(pl.multiple_of(base, many * LANES), many * LANES))]

    received(swaps)
    for j in range(GROUP):
        rows = take[j].astype(F32)
        for q in range(len(stage)):
            stage[q, pl.ds(OWN * j, OWN), :] = rows[OWN * q : OWN * q + OWN]
    for layer in PAIR:
        for which in (GATE, UP):
            for k in range(PARTS):
                at = pl.multiple_of((GROUP * k + RING * core + z) * LANES, LANES)
                wide_out[layer, which, x, y, :, pl.ds(at, LANES)] = stage[packed_row(layer, which, k) // OWN].astype(BF16)
    sent(swaps)
    own.wait()

    def spot(k, turn, by):
        out = []
        for a in AXES:
            its = (k - 1 - a) % PARTS
            out.append(None if its < turn else around(coords[a] + by) if its == turn else coords[a])
        return out

    shares = []

    def share(which, k, layer, turn, by, n):
        ref = piece(which, k, layer, spot(k, turn, by))
        shares.append(remote(ref, ref, c_send.at[k, turn, which, n], c_recv.at[k, turn, which, n], partner))
        shares[-1].start()

    everything = [(which, k, side, by) for which in (GATE, UP, DOWN) for k in range(PARTS) for side, by in SIDES]
    for turn in AXES:

        def copy(which, k, by, n, layer, start):
            ref = piece(which, k, layer, spot(k, turn, start))
            sems = send.at[k, turn, which, n], recv.at[k, turn, which, n]
            return remote(ref, ref, *sems, device(moved(coords, (k - 1 - turn) % PARTS, by), core))

        first = [copy(which, k, by, side, side, 0) for which, k, side, by in everything]
        other = [copy(which, k, by, 2 + side, 1 - side, 0) for which, k, side, by in everything]
        far = [copy(which, k, by, 4 + side, side, -by) for which, k, side, by in everything]
        begin(first)
        begin(other)
        if turn == 0:
            for which, k, side, by in everything:
                share(which, k, side, turn, 0, side)
        for n, (which, k, side, by) in enumerate(everything):
            first[n].wait_recv()
            far[n].start()
            share(which, k, side, turn, -by, 2 + side)
        for n, (which, k, side, by) in enumerate(everything):
            other[n].wait_recv()
            share(which, k, 1 - side, turn, -by, 4 + side)
        for n, (which, k, side, by) in enumerate(everything):
            far[n].wait_recv()
            share(which, k, side, turn, 2, 6 + side)
        sent(first + other + far)
    end(shares)


def all_gather(rows, down):
    owners = (*TORUS, CORES, ROWS)
    return pl.pallas_call(
        gather_kernel,
        out_shape=(
            pltpu.VMEM((LAYERS, len(PAIR), RING, RING, ROWS, FF), BF16),
            pltpu.VMEM((*owners, D), BF16),
            pltpu.VMEM((*owners, D - LANES), BF16),
            jax.ShapeDtypeStruct((*owners, LANES), BF16),
        ),
        in_specs=[VMEM] * 2,
        out_specs=(VMEM, VMEM, VMEM, ANY),
        scratch_shapes=[
            pltpu.VMEM(rows.shape, BF16),
            pltpu.VMEM((LAYERS * len(PAIR) * PARTS, ROWS, LANES), F32),
            *[DMA((GROUP,))] * 2,
            DMA,
            *[DMA((PARTS, PARTS, PARTS, 6))] * 2,
            *[DMA((PARTS, PARTS, PARTS, 8))] * 2,
        ],
        compiler_params=PARAMS(collective_id=1, has_side_effects=True, vmem_limit_bytes=mib(4)),
        name="all_gather",
    )(rows, down)


def put_kernel(wide_ref, down0_ref, down1_ref, last_ref, gate_out, up_out, down_out, bounce, sems):
    def into(ref, start, n):
        return ref.at[(1, *(ALL for _ in bounce.shape[:-1]), pl.ds(start, n))]

    pairs = [(wide_ref.at[layer, which], out.at[layer]) for layer in PAIR for which, out in ((GATE, gate_out), (UP, up_out))]
    pairs += [(down0_ref, down_out.at[0]), (down1_ref, into(down_out, 0, D - LANES))]
    pairs += [(last_ref, bounce), (bounce, into(down_out, D - LANES, LANES))]
    *copies, come, go = [pltpu.make_async_copy(src, dst, sems.at[n]) for n, (src, dst) in enumerate(pairs)]
    come.start()
    begin(copies)
    come.wait()
    go.start()
    end(copies)
    go.wait()


def put(wide, down0, down1, last):
    wide_shape = jax.ShapeDtypeStruct((LAYERS, *wide.shape[2:]), BF16)
    return pl.pallas_call(
        put_kernel,
        out_shape=(wide_shape, wide_shape, jax.ShapeDtypeStruct((LAYERS, *down0.shape), BF16)),
        in_specs=[VMEM, VMEM, VMEM, ANY],
        out_specs=(ANY, ANY, ANY),
        scratch_shapes=[pltpu.VMEM(last.shape, BF16), DMA((GROUP,))],
        compiler_params=PARAMS(vmem_limit_bytes=mib(4)),
        name="put",
    )(wide, down0, down1, last)


def nn(a, b):
    return jnp.dot(a, b, preferred_element_type=F32)


def nt(a, b):
    return lax.dot_general(a, b, (((1,), (1,)), ((), ())), preferred_element_type=F32)


def tn(a, b):
    return lax.dot_general(a, b, (((0,), (0,)), ((), ())), preferred_element_type=F32)


def rms(wide):
    return lax.rsqrt(jnp.mean(wide * wide, -1, keepdims=True) + 1e-6)


def sigmoid(g):
    return 0.5 * jnp.tanh(0.5 * g) + 0.5


def strips():
    return [pl.ds(r, STRIP) for r in range(0, T, STRIP)]


def backwards(g, u, d):
    d = d.astype(BF16).astype(F32)
    sig = sigmoid(g)
    silu = g * sig
    return (d * u * (sig + silu * (1 - sig))).astype(BF16), (d * silu).astype(BF16), silu


def forward_kernel(x_ref, wg_ref, wu_ref, wd_ref, g_ref, u_ref, act_ref, h_ref, a0t_ref, a1_ref, a1t_ref,
                   a0, wg, wu, wd, gate, up, act, w_sem, d_sem, g_sem, a_sem):
    def weights(j):
        s = slot(j)
        return [pltpu.make_async_copy(ref.at[0, :, columns(j)], buf.at[s], w_sem.at[n, s]) for n, (ref, buf) in enumerate(((wg_ref, wg), (wu_ref, wu)))]

    def downs(n):
        return [pltpu.make_async_copy(wd_ref.at[0, :, columns(n, LANES)], wd.at[slot(n)], d_sem.at[slot(n)])]

    def stores(j):
        s = slot(j)
        out = [pltpu.make_async_copy(buf.at[s], ref.at[:, columns(j)], g_sem.at[n, s]) for n, (ref, buf) in enumerate(((g_ref, gate), (u_ref, up)))]
        return out + [pltpu.make_async_copy(act.at[:, columns(j)], act_ref.at[:, columns(j)], a_sem.at[s])]

    def norm(from_ref, to_ref, turned_ref):
        @loop(T // STRIP)
        def _(i):
            rows = columns(i, STRIP)
            wide = from_ref[rows, :].astype(F32)
            a = (wide * rms(wide)).astype(BF16)
            to_ref[rows, :] = a
            turned_ref[:, rows] = a.T

    begin(weights(0))
    begin(downs(0))
    norm(x_ref, a0, a0t_ref)

    @loop(N_J)
    def _(j):
        s = slot(j)
        end(weights(j))

        @pl.when(j >= AHEAD)
        def _():
            end(stores(j - AHEAD))

        @pl.when(j + 1 < N_J)
        def _():
            begin(weights(j + 1))

        for rows in strips():
            g = nn(a0[rows, :], wg[s])
            u = nn(a0[rows, :], wu[s])
            gate[s, rows, :] = g
            up[s, rows, :] = u
            act[rows, columns(j)] = (g * sigmoid(g) * u).astype(BF16)
        begin(stores(j))

    @loop(D // LANES)
    def _(n):
        end(downs(n))

        @pl.when(n + 1 < D // LANES)
        def _():
            begin(downs(n + 1))

        for r in range(0, T, NB):
            rows = pl.ds(r, NB)
            y = nn(act[rows, :], wd[slot(n)]).astype(BF16)
            h_ref[rows, columns(n, LANES)] = x_ref[rows, columns(n, LANES)] + y

    norm(h_ref, a1_ref, a1t_ref)
    for j in PAIR:
        end(stores(N_J - AHEAD + j))


def shaped(dtype, *shapes):
    return tuple(jax.ShapeDtypeStruct(s, dtype) for s in shapes)


def slots(dtype, *shapes):
    return [pltpu.VMEM((len(PAIR), *s), dtype) for s in shapes]


def forward(x, *weights):
    two = len(PAIR)
    return pl.pallas_call(
        forward_kernel,
        out_shape=(*shaped(F32, (T, FF), (T, FF)), *shaped(BF16, (T, FF), (T, D), (D, T), (T, D), (D, T))),
        in_specs=[VMEM, ANY, ANY, ANY],
        out_specs=(ANY, ANY, ANY, VMEM, VMEM, VMEM, VMEM),
        scratch_shapes=[
            pltpu.VMEM((T, D), BF16),
            *slots(BF16, (D, NB), (D, NB), (FF, LANES)),
            *slots(F32, (T, NB), (T, NB)),
            pltpu.VMEM((T, FF), BF16),
            DMA((two, two)),
            DMA((two,)),
            DMA((two, two)),
            DMA((two,)),
        ],
        cost_estimate=pl.CostEstimate(flops=6 * T * D * FF, bytes_accessed=mib(100), transcendentals=T * FF),
        compiler_params=PARAMS(vmem_limit_bytes=mib(62)),
        name="forward",
    )(x, *weights)


def both_of(a, b):
    return tuple(enumerate(zip(a, b, strict=True)))


def tiles_of(layer, wide_refs, down_ref, wide_bufs, down_buf, sem):
    def copies(j):
        s = slot(j)
        wide = [pltpu.make_async_copy(ref.at[layer, :, columns(j)], buf.at[s], sem.at[n, s]) for n, (ref, buf) in both_of(wide_refs, wide_bufs)]
        return wide + [pltpu.make_async_copy(down_ref.at[layer, columns(j)], down_buf.at[s], sem.at[DOWN, s])]

    return copies


def wide_outs(grad_ref, first, bufs, sem):
    def copies(j):
        s, q = slot(j), j % EACH
        u = first + len(PAIR) * (j // EACH)
        return [pltpu.make_async_copy(buf.at[s], grad_ref.at[u + n, q // CORES, q % CORES], sem.at[n, s]) for n, buf in enumerate(bufs)]

    return copies


def wide_terms(at_ref, terms, bufs, s):
    for _n, (src, dst) in both_of(terms, bufs):
        w = nn(at_ref[:], src[:]).astype(BF16)
        for z in range(RING):
            dst[s, :, :, z] = w[:, z * HALF : (z + 1) * HALF].reshape(RING, RING, ROWS, HALF)


def down_loop(grad_ref, first, act_hbm, d_ref, act, out, a_sem, d_sem):
    tiles = FF // D

    def comes(t):
        return [pltpu.make_async_copy(act_hbm.at[:, columns(t, D)], act.at[slot(t)], a_sem.at[slot(t)])]

    def goes(t):
        s = slot(t)
        x, y = t // len(PAIR), pair_of(s)
        return [pltpu.make_async_copy(out.at[s, h], grad_ref.at[first + h, :, :, x, y], d_sem.at[h, s]) for h in PAIR]

    begin(comes(0))

    @loop(tiles)
    def _(t):
        s = slot(t)
        end(comes(t))

        @pl.when(t >= AHEAD)
        def _():
            end(goes(t - AHEAD))

        @pl.when(t + 1 < tiles)
        def _():
            begin(comes(t + 1))

        w = tn(act[s], d_ref[:]).astype(BF16).reshape(len(PAIR), RING, CORES, ROWS, D)
        for h in PAIR:
            for k in range(PARTS):
                at = (h * PARTS + k) * HALF
                for c in range(CORES):
                    out[s, h, k, c] = w[:, :, c, :, at : at + HALF]
        begin(goes(t))

    for t in PAIR:
        end(goes(tiles - AHEAD + t))


def layer1_kernel(a1_ref, a1t_ref, dy_ref, wg_ref, wu_ref, wd_ref, grad_ref, act1_ref, dg_ref, du_ref,
                  wg, wu, wd, act, dgate, dup, out_g, out_u, out_d, w_sem, o_sem, d_sem, a_sem, t_sem):
    weights = tiles_of(1, (wg_ref, wu_ref), wd_ref, (wg, wu), wd, w_sem)
    outs = wide_outs(grad_ref, 0, (out_g, out_u), o_sem)

    def back(j):
        pairs = both_of((dgate, dup, act.at[0, :, pl.ds(0, NB)]), (dg_ref, du_ref, act1_ref))
        return [pltpu.make_async_copy(src, dst.at[:, columns(j)], t_sem.at[n]) for n, (src, dst) in pairs]

    begin(weights(0))

    @loop(N_J)
    def _(j):
        s = slot(j)
        end(weights(j))

        @pl.when(j >= 1)
        def _():
            end(back(j - 1))

        @pl.when(j >= AHEAD)
        def _():
            end(outs(j - AHEAD))

        @pl.when(j + 1 < N_J)
        def _():
            begin(weights(j + 1))

        for rows in strips():
            g = nn(a1_ref[rows, :], wg[s])
            u = nn(a1_ref[rows, :], wu[s])
            dgate[rows, :], dup[rows, :], silu = backwards(g, u, nt(dy_ref[rows, :], wd[s]))
            act[0, rows, pl.ds(0, NB)] = (silu * u).astype(BF16)
        wide_terms(a1t_ref, (dgate, dup), (out_g, out_u), s)
        begin(back(j))
        begin(outs(j))

    end(back(N_J - 1))
    for j in PAIR:
        end(outs(N_J - AHEAD + j))
    down_loop(grad_ref, RING, act1_ref, dy_ref, act, out_d, a_sem, d_sem)


def layer0_kernel(a0t_ref, h_ref, dy_ref, wg_ref, wu_ref, wd_ref, g_ref, u_ref, act0_ref, dg_ref, du_ref,
                  grad_ref,
                  wg, wu, wd, act, dgate, dup, out_g, out_u, out_d, gate, up, total, dh,
                  w_sem, o_sem, d_sem, a_sem, l_sem, t_sem):
    weights = tiles_of(0, (wg_ref, wu_ref), wd_ref, (wg, wu), wd, w_sem)
    outs = wide_outs(grad_ref, len(PAIR), (out_g, out_u), o_sem)
    sources = list(zip((dg_ref, du_ref), (wg_ref, wu_ref), (dgate, dup), (wg, wu), strict=True))

    def da_in(j, which):
        d_from, w_from, d_to, w_to = sources[which]
        s = slot(j)
        return [pltpu.make_async_copy(d_from.at[:, columns(j)], d_to, t_sem.at[which]),
                pltpu.make_async_copy(w_from.at[1, :, columns(j)], w_to.at[s], w_sem.at[which, s])]

    for which in PAIR:
        begin(da_in(0, which))
    total[:] = jnp.zeros_like(total)

    @loop(N_J)
    def _(j):
        for which in PAIR:
            end(da_in(j, which))
            d_to, w_to = sources[which][len(PAIR) :]
            for rows in strips():
                total[which, rows, :] += nt(d_to[rows, :], w_to[slot(j)])

            @pl.when(j + 1 < N_J)
            def _(which=which):
                begin(da_in(j + 1, which))

    begin(weights(0))

    @loop(T // STRIP)
    def _(i):
        rows = columns(i, STRIP)
        wide = h_ref[rows, :].astype(F32)
        scale = rms(wide)
        da = sum(total[which, rows, :].astype(BF16) for which in PAIR).astype(F32)
        mean = jnp.mean(da * wide, -1, keepdims=True)
        d = da * scale - wide * (mean * scale * scale * scale)
        dh[rows, :] = dy_ref[rows, :] + d.astype(BF16)

    down_loop(grad_ref, 0, act0_ref, dh, act, out_d, a_sem, d_sem)

    def products(j):
        s = slot(j)
        return [pltpu.make_async_copy(ref.at[:, columns(j)], buf.at[s], l_sem.at[n, s]) for n, (ref, buf) in both_of((g_ref, u_ref), (gate, up))]

    begin(products(0))

    @loop(N_J)
    def _(j):
        s = slot(j)
        end(weights(j))
        end(products(j))

        @pl.when(j >= AHEAD)
        def _():
            end(outs(j - AHEAD))

        @pl.when(j + 1 < N_J)
        def _():
            begin(weights(j + 1))
            begin(products(j + 1))

        for rows in strips():
            dgate[rows, :], dup[rows, :], _silu = backwards(gate[s, rows, :], up[s, rows, :], nt(dh[rows, :], wd[s]))
        wide_terms(a0t_ref, (dgate, dup), (out_g, out_u), s)
        begin(outs(j))

    for j in PAIR:
        end(outs(N_J - AHEAD + j))


def scatter_kernel(grad_ref, grad1_ref, take_ref, own_ref, ss_ref, *scratch):
    sc, rest = scatter_of((grad_ref, grad1_ref), scratch)
    enter(sc.coords, sc.core)
    sc.squares[:] = jnp.zeros_like(sc.squares)
    sc.feed(0)
    sc.feed(1)
    sc.add(0)

    @loop(UNITS + AHEAD)
    def _(i):
        sc.middles(i)

        @pl.when(i + 1 < UNITS)
        def _():
            sc.add(i + 1)

        sc.finishes(i)

        @pl.when(i + AHEAD < UNITS)
        def _():
            sc.feed(i + AHEAD)

    last_swap(sc, take_ref, own_ref, ss_ref, *rest)


TWO = len(PAIR)
OUT_TILE = (*TORUS, *CELL)
GRAD = (EACH, PARTS, CORES, *OUT_TILE)


def tile_buffers():
    return [
        *slots(BF16, (D, NB), (D, NB), (NB, D), (T, D)),
        *[pltpu.VMEM((T, NB), BF16)] * 2,
        *slots(BF16, OUT_TILE, OUT_TILE, (TWO, PARTS, CORES, TWO, RING, *CELL)),
    ]


def tile_semaphores():
    return [DMA((PARTS, TWO)), DMA((TWO, TWO)), DMA((TWO, TWO)), DMA((TWO,))]


def layer1(a1, a1t, dy, *weights):
    return pl.pallas_call(
        layer1_kernel,
        out_shape=shaped(BF16, GRAD, (T, FF), (T, FF), (T, FF)),
        in_specs=[VMEM] * 3 + [ANY] * 3,
        out_specs=(ANY,) * 4,
        scratch_shapes=[*tile_buffers(), *tile_semaphores(), DMA((PARTS,))],
        cost_estimate=pl.CostEstimate(flops=12 * T * D * FF, bytes_accessed=mib(120), transcendentals=T * FF),
        compiler_params=PARAMS(vmem_limit_bytes=mib(62)),
        name="layer1",
    )(a1, a1t, dy, *weights)


def layer0(*args):
    return pl.pallas_call(
        layer0_kernel,
        out_shape=jax.ShapeDtypeStruct(GRAD, BF16),
        in_specs=[VMEM] * 3 + [ANY] * 8,
        out_specs=ANY,
        scratch_shapes=[
            *tile_buffers(),
            *slots(F32, (T, NB), (T, NB), (T, D)),
            pltpu.VMEM((T, D), BF16),
            *tile_semaphores(),
            DMA((TWO, TWO)),
            DMA((PARTS,)),
        ],
        cost_estimate=pl.CostEstimate(flops=12 * T * D * FF, bytes_accessed=mib(200), transcendentals=T * FF),
        compiler_params=PARAMS(vmem_limit_bytes=mib(62)),
        name="layer0",
    )(*args)


def reduce_scatter(*grads):
    return pl.pallas_call(
        scatter_kernel,
        out_shape=(*shaped(BF16, (GROUP, PACKED, LANES)), *shaped(F32, (LAYERS, ROWS, D), (8, HALF))),
        in_specs=[ANY] * 2,
        out_specs=(VMEM,) * 3,
        scratch_shapes=scatter_scratch(),
        compiler_params=PARAMS(collective_id=0, has_side_effects=True, vmem_limit_bytes=mib(60)),
        name="reduce_scatter",
    )(*grads)


def adamw(w, m, v, g):
    m = 0.9 * m + 0.1 * g
    v = 0.95 * v + 0.05 * g * g
    step = m * lax.rsqrt(v + 1e-8) + 0.1 * w
    return w - 0.02 * step, m, v


def optimizer_kernel(count, take_ref, down_g_ref, squares_ref, wg_ref, wu_ref, wd_ref, mg_ref, mu_ref, md_ref, vg_ref, vu_ref, vd_ref,
                     send_ref, down_ref, mg_out, mu_out, md_out, vg_out, vu_out, vd_out, near, down_w, takes, g6, sends, sems):
    coords, core = place()
    x, y, z = coords
    copies = []
    for which, ref in enumerate((wg_ref, wu_ref)):
        copies.append(pltpu.make_async_copy(ref.at[:, pl.ds((RING * x + y) * ROWS, ROWS)], near.at[which], sems.at[which]))
    copies.append(pltpu.make_async_copy(wd_ref.at[:, pl.ds(number(coords, core) * ROWS, ROWS)], down_w, sems.at[DOWN]))
    begin(copies)
    squares = jnp.sum(jnp.sum(squares_ref[:], axis=0, keepdims=True), axis=1, keepdims=True)
    factor = jnp.minimum(1.0, 0.5 * lax.rsqrt(squares / count + 1e-30))
    takes[:] = take_ref[:].astype(F32)
    sends[:] = jnp.zeros_like(sends)
    end(copies)

    rows = lax.broadcasted_iota(jnp.int32, (GROUP, ROWS), 0)
    among = lax.broadcasted_iota(jnp.int32, (GROUP, ROWS), 1)
    sel = ((among == OWN * (CORES * z + core) + rows) & (rows < OWN)).astype(F32).astype(BF16)
    places = [(k, c, zz) for k in range(PARTS) for c in range(CORES) for zz in range(RING)]
    moments = ((mg_ref, vg_ref, mg_out, vg_out), (mu_ref, vu_ref, mu_out, vu_out))
    for layer in PAIR:
        for which in (GATE, UP):
            for half in PAIR:
                for n, (k, c, zz) in enumerate(places):
                    row = packed_row(layer, which, k)
                    g6[:, lanes(half * len(places) + n)] = takes[CORES * zz + c, pl.ds(row, OWN), lanes(half)]
            w = nn(sel, near[which, layer])[:OWN]
            m_in, v_in, m_out, v_out = moments[which]
            w, m_out[:, layer, :], v_out[:, layer, :] = adamw(w, m_in[:, layer, :], v_in[:, layer, :], g6[:] * factor)
            for n, (k, c, zz) in enumerate(places):
                sends[CORES * zz + c, pl.ds(packed_row(layer, which, k), OWN), :] = w[:, n * LANES : (n + 1) * LANES]
    send_ref[:] = sends[:].astype(BF16)
    for layer in PAIR:
        w, md_out[layer], vd_out[layer] = adamw(down_w[layer].astype(F32), md_ref[layer], vd_ref[layer], down_g_ref[layer] * factor)
        down_ref[layer] = w.astype(BF16)


def optimizer(sums, weights, m, v):
    shapes = shaped(F32, *(t.shape for t in m))
    packed = (GROUP, PACKED, LANES)
    return pl.pallas_call(
        functools.partial(optimizer_kernel, sum(w.size for w in weights)),
        out_shape=(*shaped(BF16, packed, (LAYERS, ROWS, D)), *shapes, *shapes),
        in_specs=[VMEM] * 3 + [ANY] * 3 + [VMEM] * 6,
        out_specs=(VMEM,) * 8,
        scratch_shapes=[
            *slots(BF16, (LAYERS, ROWS, FF), (ROWS, D)),
            pltpu.VMEM(packed, F32),
            pltpu.VMEM((OWN, FF), F32),
            pltpu.VMEM(packed, F32),
            DMA((PARTS,)),
        ],
        compiler_params=PARAMS(vmem_limit_bytes=mib(62)),
        name="optimizer",
    )(*sums, *weights, *m, *v)


def turned(moments):
    gate, up, down = moments
    return [gate.swapaxes(0, 1), up.swapaxes(0, 1), down]


def terms(x, dy, weights):
    g, u, act0, h, a0t, a1, a1t = forward(x, *weights)
    grad1, _act1, dg, du = layer1(a1, a1t, dy, *weights)
    return grad1, layer0(a0t, h, dy, *weights, g, u, act0, dg, du)


def local_step(x, dy, *arrays):
    weights, m, v = (arrays[i : i + PARTS] for i in range(0, len(arrays), PARTS))
    grad1, grad0 = terms(x[0], dy[0], weights)
    sums = reduce_scatter(grad0, grad1)
    send, down, *new = optimizer(sums, weights, turned(m), turned(v))
    spaces = (pltpu.VMEM, pltpu.VMEM, pltpu.VMEM, pltpu.HBM)
    gathered = all_gather(send, down)
    new_weights = put(*(pltpu.with_memory_space_constraint(w, space) for w, space in zip(gathered, spaces, strict=True)))
    return (*(n.reshape(w.shape) for n, w in zip(new_weights, weights, strict=True)), *turned(new[:PARTS]), *turned(new[PARTS:]))


def solution(mesh):
    moments = P(None, "dp", None)
    whole, mine = P(), P("dp")
    return jax.shard_map(
        local_step,
        mesh=mesh,
        in_specs=(mine, mine, whole, whole, whole, *(moments,) * 6),
        out_specs=(whole, whole, whole, *(moments,) * 6),
        check_vma=False,
    )
```

time: 2310 us -> 512 us (0.22); the launches traced: 2280 us -> 510 us
  blocking collectives: 931 us -> 0 us
  Pallas kernels: 0 us -> 510 us
  local copies, waits for them, and re-layouts: 430 us -> 0 us
  starting transfers between devices: 346 us -> 0 us
  matrix products: 293 us -> 0 us
  waiting for transfers between devices: 205 us -> 0 us
  other arithmetic: 55.4 us -> 0 us
    unnamed x2 -> x0, blocking collectives: 868 us -> none
    pallas_call x0 -> x7, Pallas kernels: none -> 510 us  [the longest x1 148 us: reduce_scatter(): pl.pallas_call(scatter_kernel, out_shape=(*shaped(BF16, (GROUP, PACKED, L...]
    unnamed x149 -> x0, local copies, waits for them, and re-layouts: 426 us -> none
    unnamed x130 -> x0, starting transfers between devices: 346 us -> none
    dot_general x15 -> x0, matrix products: 293 us -> none  [the longest x5 104 us: layer(): up = jnp.dot(a, w['w_up'], preferred_element_type=jnp.float32)]
    reshape x3 -> x0, waiting for transfers between devices: 203 us -> none  [step(): t.reshape(-1, *t.shape[2:])]
    reduce_sum x1 -> x0, blocking collectives: 62.7 us -> none  [of_a_group(): jnp.sum(g * g)]
    unnamed x7 -> x0, other arithmetic: 44.8 us -> none
  transfers between devices with their start and end apart: 133 -> 0, of which waited for: 4 -> 0; matrix products, arithmetic and copies ran while one was open for 62% -> 0% of each run, Pallas kernels for 0% -> 0%
where the time goes in v1:
time: 512 us; the launch traced here: 510 us
  Pallas kernels  510 us (100%)
    pallas_call x1, Pallas kernels, reduce_scatter(): pl.pallas_call(scatter_kernel, out_shape=(*shaped(BF16, (GROUP, PACKED, L...  148 us
    pallas_call x1, Pallas kernels, all_gather(): pl.pallas_call(gather_kernel, out_shape=(pltpu.VMEM((LAYERS, len(PAIR), R...  127 us
    pallas_call x1, Pallas kernels, layer0(): pl.pallas_call(layer0_kernel, out_shape=jax.ShapeDtypeStruct(GRAD, BF16),...  89.7 us
    pallas_call x1, Pallas kernels, layer1(): pl.pallas_call(layer1_kernel, out_shape=shaped(BF16, GRAD, (T, FF), (T, F...  75.2 us
    pallas_call x1, Pallas kernels, forward(): pl.pallas_call(forward_kernel, out_shape=(*shaped(F32, (T, FF), (T, FF)),...  45 us
    pallas_call x1, Pallas kernels, put(): pl.pallas_call(put_kernel, out_shape=(wide_shape, wide_shape, jax.ShapeDt...  18.5 us

profile of v1, /device:TPU:1, one launch (start us, length us, event | category | flops | bytes accessed | tf_op | source)
XLA Modules:
  0.0 510.4 jit_solution(13101876220075879659)
XLA Ops:
  0.6 45.0 %forward.1 = (f32[1024,6144]{1,0:T(8,128)}, f32[1024,6144]{1,0:T(8,128)}, bf16[1024,6144]{1,0:T(8,128)(2,1)}, bf16[1024,768]{1,0:T(8,128)(2,1)}, bf16[768,1024]{...) custom-call(bf16[1024,768]{1,0:T(8,128)(2,1)} %bitcast.20, bf16[2,768,6144]{2,1,0:T(8,128)(2,1)} %wg_ref.7, ...), custom_call_target="tpu_custom_call" | custom-call | flops 28991029248 | bytes 104857600 | tf_op jit(solution)/shard_map/forward/pallas_call | solution.py:653
  45.7 75.2 %layer1.1 = (bf16[6,3,2,4,4,4,48,128]{7,6,5,4,3,2,1,0:T(8,128)(2,1)}, bf16[1024,6144]{1,0:T(8,128)(2,1)}, bf16[1024,6144]{1,0:T(8,128)(2,1)}, bf16[1024,6144]{1,0:T(8,128)(2,1)}) custom-call(bf16[1024,768]{1,0:T(8,128)(2,1)} %get-tuple-element.42.a1_ref, bf16[768,1024]{1,0:T(8,128)(2,1)} %get-tuple-element.43.a1t_ref, bf16[1024,768]{1,0:T(8,128)(2,1)} %bitcast.21, ...), custom_call_target="tpu_custom_call" | custom-call | flops 57982058496 | bytes 125829120 | tf_op jit(solution)/shard_map/layer1/pallas_call | solution.py:901
  120.8 89.7 %layer0.1.grad_ref = bf16[6,3,2,4,4,4,48,128]{7,6,5,4,3,2,1,0:T(8,128)(2,1)} custom-call(bf16[768,1024]{1,0:T(8,128)(2,1)} %get-tuple-element.37.a0t_ref, bf16[1024,768]{1,0:T(8,128)(2,1)} %get-tuple-element.38.h_ref, bf16[1024,768]{1,0:T(8,128)(2,1)} %bitcast.22, bf16[2,768,6144]{2,1,0:T(8,128)(2,1)} %wg_ref.7, bf16[2,768,6144]{2,1,0:T(8,128)(2,1)} %wu_ref.7, ...), custom_call_target="tpu_custom_call" | custom-call | flops 57982058496 | bytes 209715200 | tf_op jit(solution)/shard_map/layer0/pallas_call | solution.py:914
  210.6 147.8 %reduce_scatter.1 = (bf16[8,80,256]{2,1,0:T(8,128)(2,1)}, f32[2,48,768]{2,1,0:T(8,128)}, f32[8,128]{1,0:T(8,128)}) custom-call(bf16[6,3,2,4,4,4,48,128]{7,6,5,4,3,2,1,0:T(8,128)(2,1)} %layer0.1.grad_ref, bf16[6,3,2,4,4,4,48,128]{7,6,5,4,3,2,1,0:T(8,128)(2,1)} %get-tuple-element.46.grad1_ref), custom_call_target="tpu_custom_call" | custom-call | tf_op jit(solution)/shard_map/reduce_scatter/pallas_call | solution.py:934
  358.3 5.9 %optimizer.1 = (bf16[8,80,256]{2,1,0:T(8,128)(2,1)}, bf16[2,48,768]{2,1,0:T(8,128)(2,1)}, f32[6,2,6144]{2,1,0:T(2,128)}, f32[6,2,6144]{2,1,0:T(2,128)}, f32[2,48...) custom-call(bf16[8,80,256]{2,1,0:T(8,128)(2,1)} %get-tuple-element.47.take_ref, ...), custom_call_target="tpu_custom_call" | custom-call | tf_op jit(solution)/shard_map/optimizer/pallas_call | solution.py:992
  364.3 127.5 %all_gather.1 = (bf16[2,2,4,4,48,6144]{5,4,3,2,1,0:T(8,128)(2,1)S(1)}, bf16[4,4,4,2,48,768]{5,4,3,2,1,0:T(8,128)(2,1)S(1)}, bf16[4,4,4,2,48,512]{5,4,3,2,1,0:T(8,128)(2,1)S(1)}, bf16[4,4,4,2,48,256]{5,4,3,2,1,0:T(8,128)(2,1)}) custom-call(bf16[8,80,256]{2,1,0:T(8,128)(2,1)} %get-tuple-element.50.rows_ref, bf16[2,48,768]{2,1,0:T(8,128)(2,1)} %get-tuple-element.51.down_ref), custom_call_target="tpu_custom_call" | custom-call | tf_op jit(solution)/shard_map/all_gather/pallas_call | solution.py:494
  491.7 18.5 %put.1 = (bf16[2,4,4,48,6144]{4,3,2,1,0:T(8,128)(2,1)}, bf16[2,4,4,48,6144]{4,3,2,1,0:T(8,128)(2,1)}, bf16[2,4,4,4,2,48,768]{6,5,4,3,2,1,0:T(8,128)(2,1)}) custom-call(bf16[2,2,4,4,48,6144]{5,4,3,2,1,0:T(8,128)(2,1)S(1)} %get-tuple-element.52.wide_ref, bf16[4,4,4,2,48,768]{5,4,3,2,1,0:T(8,128)(2,1)S(1)} %get-tuple-element.53.down0_ref, ...), custom_call_target="tpu_custom_call" | custom-call | tf_op jit(solution)/shard_map/put/pallas_call | solution.py:535

commit v2 on v1

--- a/solution.py
+++ b/solution.py
@@ -567,14 +567,13 @@
     return [pl.ds(r, STRIP) for r in range(0, T, STRIP)]
 
 
-def backwards(g, u, d):
-    d = d.astype(BF16).astype(F32)
+def factors(g, u):
     sig = sigmoid(g)
     silu = g * sig
-    return (d * u * (sig + silu * (1 - sig))).astype(BF16), (d * silu).astype(BF16), silu
-
-
-def forward_kernel(x_ref, wg_ref, wu_ref, wd_ref, g_ref, u_ref, act_ref, h_ref, a0t_ref, a1_ref, a1t_ref,
+    return u * (sig + silu * (1 - sig)), silu, (silu * u).astype(BF16)
+
+
+def forward_kernel(x_ref, wg_ref, wu_ref, wd_ref, g_ref, u_ref, act_ref, h_ref, scale_ref, a0t_ref, a1_ref, a1t_ref,
                    a0, wg, wu, wd, gate, up, act, w_sem, d_sem, g_sem, a_sem):
     def weights(j):
         s = slot(j)
@@ -593,7 +592,9 @@
         def _(i):
             rows = columns(i, STRIP)
             wide = from_ref[rows, :].astype(F32)
-            a = (wide * rms(wide)).astype(BF16)
+            scale = rms(wide)
+            scale_ref[rows, :] = jnp.broadcast_to(scale, (STRIP, HALF))
+            a = (wide * scale).astype(BF16)
             to_ref[rows, :] = a
             turned_ref[:, rows] = a.T
 
@@ -615,11 +616,7 @@
             begin(weights(j + 1))
 
         for rows in strips():
-            g = nn(a0[rows, :], wg[s])
-            u = nn(a0[rows, :], wu[s])
-            gate[s, rows, :] = g
-            up[s, rows, :] = u
-            act[rows, columns(j)] = (g * sigmoid(g) * u).astype(BF16)
+            gate[s, rows, :], up[s, rows, :], act[rows, columns(j)] = factors(nn(a0[rows, :], wg[s]), nn(a0[rows, :], wu[s]))
         begin(stores(j))
 
     @loop(D // LANES)
@@ -652,9 +649,9 @@
     two = len(PAIR)
     return pl.pallas_call(
         forward_kernel,
-        out_shape=(*shaped(F32, (T, FF), (T, FF)), *shaped(BF16, (T, FF), (T, D), (D, T), (T, D), (D, T))),
+        out_shape=(*shaped(F32, (T, FF), (T, FF)), *shaped(BF16, (T, FF), (T, D)), *shaped(F32, (T, HALF)), *shaped(BF16, (D, T), (T, D), (D, T))),
         in_specs=[VMEM, ANY, ANY, ANY],
-        out_specs=(ANY, ANY, ANY, VMEM, VMEM, VMEM, VMEM),
+        out_specs=(ANY,) * 3 + (VMEM,) * 5,
         scratch_shapes=[
             pltpu.VMEM((T, D), BF16),
             *slots(BF16, (D, NB), (D, NB), (FF, LANES)),
@@ -694,15 +691,16 @@
 
 
 def wide_terms(at_ref, terms, bufs, s):
-    for _n, (src, dst) in both_of(terms, bufs):
-        w = nn(at_ref[:], src[:]).astype(BF16)
+    for n, dst in enumerate(bufs):
+        w = nn(at_ref[:], terms[s, n]).astype(BF16)
         for z in range(RING):
             dst[s, :, :, z] = w[:, z * HALF : (z + 1) * HALF].reshape(RING, RING, ROWS, HALF)
 
 
-def down_loop(grad_ref, first, act_hbm, d_ref, act, out, a_sem, d_sem):
-    tiles = FF // D
-
+TILES = FF // D
+
+
+def down_parts(grad_ref, first, act_hbm, d_ref, act, out, a_sem, d_sem):
     def comes(t):
         return [pltpu.make_async_copy(act_hbm.at[:, columns(t, D)], act.at[slot(t)], a_sem.at[slot(t)])]
 
@@ -711,10 +709,7 @@
         x, y = t // len(PAIR), pair_of(s)
         return [pltpu.make_async_copy(out.at[s, h], grad_ref.at[first + h, :, :, x, y], d_sem.at[h, s]) for h in PAIR]
 
-    begin(comes(0))
-
-    @loop(tiles)
-    def _(t):
+    def step(t):
         s = slot(t)
         end(comes(t))
 
@@ -722,7 +717,7 @@
         def _():
             end(goes(t - AHEAD))
 
-        @pl.when(t + 1 < tiles)
+        @pl.when(t + 1 < TILES)
         def _():
             begin(comes(t + 1))
 
@@ -734,18 +729,22 @@
                     out[s, h, k, c] = w[:, :, c, :, at : at + HALF]
         begin(goes(t))
 
-    for t in PAIR:
-        end(goes(tiles - AHEAD + t))
+    def finish():
+        for t in PAIR:
+            end(goes(TILES - AHEAD + t))
+
+    return comes, step, finish
 
 
 def layer1_kernel(a1_ref, a1t_ref, dy_ref, wg_ref, wu_ref, wd_ref, grad_ref, act1_ref, dg_ref, du_ref,
-                  wg, wu, wd, act, dgate, dup, out_g, out_u, out_d, w_sem, o_sem, d_sem, a_sem, t_sem):
+                  wg, wu, wd, act, terms, out_g, out_u, out_d, w_sem, o_sem, d_sem, a_sem, t_sem):
     weights = tiles_of(1, (wg_ref, wu_ref), wd_ref, (wg, wu), wd, w_sem)
     outs = wide_outs(grad_ref, 0, (out_g, out_u), o_sem)
 
     def back(j):
-        pairs = both_of((dgate, dup, act.at[0, :, pl.ds(0, NB)]), (dg_ref, du_ref, act1_ref))
-        return [pltpu.make_async_copy(src, dst.at[:, columns(j)], t_sem.at[n]) for n, (src, dst) in pairs]
+        s = slot(j)
+        pairs = both_of((terms.at[s, GATE], terms.at[s, UP], act.at[s, :, pl.ds(0, NB)]), (dg_ref, du_ref, act1_ref))
+        return [pltpu.make_async_copy(src, dst.at[:, columns(j)], t_sem.at[n, s]) for n, (src, dst) in pairs]
 
     begin(weights(0))
 
@@ -754,12 +753,9 @@
         s = slot(j)
         end(weights(j))
 
-        @pl.when(j >= 1)
-        def _():
-            end(back(j - 1))
-
         @pl.when(j >= AHEAD)
         def _():
+            end(back(j - AHEAD))
             end(outs(j - AHEAD))
 
         @pl.when(j + 1 < N_J)
@@ -767,72 +763,87 @@
             begin(weights(j + 1))
 
         for rows in strips():
-            g = nn(a1_ref[rows, :], wg[s])
-            u = nn(a1_ref[rows, :], wu[s])
-            dgate[rows, :], dup[rows, :], silu = backwards(g, u, nt(dy_ref[rows, :], wd[s]))
-            act[0, rows, pl.ds(0, NB)] = (silu * u).astype(BF16)
-        wide_terms(a1t_ref, (dgate, dup), (out_g, out_u), s)
+            by_gate, by_up, a = factors(nn(a1_ref[rows, :], wg[s]), nn(a1_ref[rows, :], wu[s]))
+            d = nt(dy_ref[rows, :], wd[s]).astype(BF16).astype(F32)
+            act[s, rows, pl.ds(0, NB)] = a
+            terms[s, GATE, rows, :] = (d * by_gate).astype(BF16)
+            terms[s, UP, rows, :] = (d * by_up).astype(BF16)
+        wide_terms(a1t_ref, terms, (out_g, out_u), s)
         begin(back(j))
         begin(outs(j))
 
-    end(back(N_J - 1))
     for j in PAIR:
+        end(back(N_J - AHEAD + j))
         end(outs(N_J - AHEAD + j))
-    down_loop(grad_ref, RING, act1_ref, dy_ref, act, out_d, a_sem, d_sem)
-
-
-def layer0_kernel(a0t_ref, h_ref, dy_ref, wg_ref, wu_ref, wd_ref, g_ref, u_ref, act0_ref, dg_ref, du_ref,
-                  grad_ref,
-                  wg, wu, wd, act, dgate, dup, out_g, out_u, out_d, gate, up, total, dh,
-                  w_sem, o_sem, d_sem, a_sem, l_sem, t_sem):
+    comes, step, finish = down_parts(grad_ref, RING, act1_ref, dy_ref, act, out_d, a_sem, d_sem)
+    begin(comes(0))
+    loop(TILES)(step)
+    finish()
+
+
+FIRST_DOWN = N_J
+FIRST_WIDE = FIRST_DOWN + TILES
+LAST_STEPS = FIRST_WIDE + N_J
+STEPS = LAST_STEPS + 6
+MIDDLES = (3, 7, 11, 17, 20, 22, 25, 28, 31, *range(LAST_STEPS + 1, STEPS))
+FINISHES = (5, 9, 13, 19, 21, 23, 26, 29, *range(LAST_STEPS, STEPS))
+FEEDS = (5, 9, 13, 19, 21, 23, 27, 29, LAST_STEPS, LAST_STEPS + 1)
+
+
+def due(step, steps, do):
+    now = functools.reduce(jnp.logical_or, [step == at for at in steps])
+    n = sum((step > at).astype(jnp.int32) for at in steps)
+
+    @pl.when(now)
+    def _():
+        do(n)
+
+
+def layer0_kernel(a0t_ref, h_ref, scale_ref, dy_ref, wg_ref, wu_ref, wd_ref, g_ref, u_ref, act0_ref, dg_ref, du_ref, grad1_ref,
+                  grad_ref, take_ref, own_ref, ss_ref,
+                  wg, wu, wd, act, terms, out_g, out_u, out_d, gate, up, total, dh,
+                  w_sem, o_sem, d_sem, a_sem, l_sem, t_sem, *scratch):
+    sc, rest = scatter_of((grad_ref, grad1_ref), scratch)
     weights = tiles_of(0, (wg_ref, wu_ref), wd_ref, (wg, wu), wd, w_sem)
     outs = wide_outs(grad_ref, len(PAIR), (out_g, out_u), o_sem)
-    sources = list(zip((dg_ref, du_ref), (wg_ref, wu_ref), (dgate, dup), (wg, wu), strict=True))
-
-    def da_in(j, which):
-        d_from, w_from, d_to, w_to = sources[which]
-        s = slot(j)
-        return [pltpu.make_async_copy(d_from.at[:, columns(j)], d_to, t_sem.at[which]),
-                pltpu.make_async_copy(w_from.at[1, :, columns(j)], w_to.at[s], w_sem.at[which, s])]
-
-    for which in PAIR:
-        begin(da_in(0, which))
-    total[:] = jnp.zeros_like(total)
-
-    @loop(N_J)
-    def _(j):
-        for which in PAIR:
-            end(da_in(j, which))
-            d_to, w_to = sources[which][len(PAIR) :]
-            for rows in strips():
-                total[which, rows, :] += nt(d_to[rows, :], w_to[slot(j)])
-
-            @pl.when(j + 1 < N_J)
-            def _(which=which):
-                begin(da_in(j + 1, which))
-
-    begin(weights(0))
-
-    @loop(T // STRIP)
-    def _(i):
-        rows = columns(i, STRIP)
-        wide = h_ref[rows, :].astype(F32)
-        scale = rms(wide)
-        da = sum(total[which, rows, :].astype(BF16) for which in PAIR).astype(F32)
-        mean = jnp.mean(da * wide, -1, keepdims=True)
-        d = da * scale - wide * (mean * scale * scale * scale)
-        dh[rows, :] = dy_ref[rows, :] + d.astype(BF16)
-
-    down_loop(grad_ref, 0, act0_ref, dh, act, out_d, a_sem, d_sem)
+    comes, down_step, down_finish = down_parts(grad_ref, 0, act0_ref, dh, act, out_d, a_sem, d_sem)
+    sources = both_of((dg_ref, du_ref), zip((wg_ref, wu_ref), (wg, wu), strict=True))
 
     def products(j):
         s = slot(j)
         return [pltpu.make_async_copy(ref.at[:, columns(j)], buf.at[s], l_sem.at[n, s]) for n, (ref, buf) in both_of((g_ref, u_ref), (gate, up))]
 
-    begin(products(0))
-
-    @loop(N_J)
-    def _(j):
+    def da_in(j):
+        s, out = slot(j), []
+        for n, (d_from, (w_from, w_to)) in sources:
+            out.append(pltpu.make_async_copy(d_from.at[:, columns(j)], terms.at[s, n], t_sem.at[n, s]))
+            out.append(pltpu.make_async_copy(w_from.at[1, :, columns(j)], w_to.at[s], w_sem.at[n, s]))
+        return out
+
+    def da_step(j):
+        s = slot(j)
+        end(da_in(j))
+
+        @pl.when(j + 1 < N_J)
+        def _():
+            begin(da_in(j + 1))
+
+        for n, (_d, (_w, w)) in sources:
+            for rows in strips():
+                total[n, rows, :] += nt(terms[s, n, rows, :], w[s])
+
+    def states_step():
+        @loop(T // STRIP)
+        def _(i):
+            rows = columns(i, STRIP)
+            wide = h_ref[rows, :].astype(F32)
+            scale = scale_ref[rows, pl.ds(0, 1)]
+            da = sum(total[n, rows, :].astype(BF16) for n in PAIR).astype(F32)
+            mean = jnp.sum(da * wide, -1, keepdims=True) * (1 / D)
+            d = da * scale - wide * (mean * scale * scale * scale)
+            dh[rows, :] = dy_ref[rows, :] + d.astype(BF16)
+
+    def wide_step(j):
         s = slot(j)
         end(weights(j))
         end(products(j))
@@ -847,35 +858,60 @@
             begin(products(j + 1))
 
         for rows in strips():
-            dgate[rows, :], dup[rows, :], _silu = backwards(gate[s, rows, :], up[s, rows, :], nt(dh[rows, :], wd[s]))
-        wide_terms(a0t_ref, (dgate, dup), (out_g, out_u), s)
+            d = nt(dh[rows, :], wd[s]).astype(BF16).astype(F32)
+            terms[s, GATE, rows, :] = (d * gate[s, rows, :]).astype(BF16)
+            terms[s, UP, rows, :] = (d * up[s, rows, :]).astype(BF16)
+        wide_terms(a0t_ref, terms, (out_g, out_u), s)
         begin(outs(j))
 
-    for j in PAIR:
-        end(outs(N_J - AHEAD + j))
-
-
-def scatter_kernel(grad_ref, grad1_ref, take_ref, own_ref, ss_ref, *scratch):
-    sc, rest = scatter_of((grad_ref, grad1_ref), scratch)
+    begin(da_in(0))
+    begin(comes(0))
+    begin(products(0))
     enter(sc.coords, sc.core)
     sc.squares[:] = jnp.zeros_like(sc.squares)
     sc.feed(0)
     sc.feed(1)
+    total[:] = jnp.zeros_like(total)
     sc.add(0)
 
-    @loop(UNITS + AHEAD)
-    def _(i):
-        sc.middles(i)
-
-        @pl.when(i + 1 < UNITS)
-        def _():
-            sc.add(i + 1)
-
-        sc.finishes(i)
-
-        @pl.when(i + AHEAD < UNITS)
-        def _():
-            sc.feed(i + AHEAD)
+    @loop(STEPS)
+    def _(step):
+        @pl.when(step < FIRST_DOWN)
+        def _():
+            da_step(step)
+
+        @pl.when(step == FIRST_DOWN - 1)
+        def _():
+            begin(weights(0))
+            states_step()
+
+        @pl.when((step >= FIRST_DOWN) & (step < FIRST_WIDE))
+        def _():
+            down_step(step - FIRST_DOWN)
+
+        @pl.when(step == FIRST_WIDE - 1)
+        def _():
+            down_finish()
+
+        @pl.when((step >= FIRST_WIDE) & (step < LAST_STEPS))
+        def _():
+            wide_step(step - FIRST_WIDE)
+
+        @pl.when(step == LAST_STEPS - 1)
+        def _():
+            for j in PAIR:
+                end(outs(N_J - AHEAD + j))
+
+        def middles_and_add(i):
+            sc.middles(i)
+
+            @pl.when(i + 1 < UNITS)
+            def _():
+                sc.add(i + 1)
+
+        due(step, MIDDLES, middles_and_add)
+        due(step, FINISHES, sc.finishes)
+        due(step, FEEDS, lambda n: sc.feed(n + AHEAD))
 
     last_swap(sc, take_ref, own_ref, ss_ref, *rest)
 
@@ -887,8 +923,7 @@
 
 def tile_buffers():
     return [
-        *slots(BF16, (D, NB), (D, NB), (NB, D), (T, D)),
-        *[pltpu.VMEM((T, NB), BF16)] * 2,
+        *slots(BF16, (D, NB), (D, NB), (NB, D), (T, D), (TWO, T, NB)),
         *slots(BF16, OUT_TILE, OUT_TILE, (TWO, PARTS, CORES, TWO, RING, *CELL)),
     ]
 
@@ -903,7 +938,7 @@
         out_shape=shaped(BF16, GRAD, (T, FF), (T, FF), (T, FF)),
         in_specs=[VMEM] * 3 + [ANY] * 3,
         out_specs=(ANY,) * 4,
-        scratch_shapes=[*tile_buffers(), *tile_semaphores(), DMA((PARTS,))],
+        scratch_shapes=[*tile_buffers(), *tile_semaphores(), DMA((PARTS, TWO))],
         cost_estimate=pl.CostEstimate(flops=12 * T * D * FF, bytes_accessed=mib(120), transcendentals=T * FF),
         compiler_params=PARAMS(vmem_limit_bytes=mib(62)),
         name="layer1",
@@ -913,33 +948,22 @@
 def layer0(*args):
     return pl.pallas_call(
         layer0_kernel,
-        out_shape=jax.ShapeDtypeStruct(GRAD, BF16),
-        in_specs=[VMEM] * 3 + [ANY] * 8,
-        out_specs=ANY,
+        out_shape=(*shaped(BF16, GRAD, (GROUP, PACKED, LANES)), *shaped(F32, (LAYERS, ROWS, D), (8, HALF))),
+        in_specs=[VMEM] * 4 + [ANY] * 9,
+        out_specs=(ANY, VMEM, VMEM, VMEM),
         scratch_shapes=[
             *tile_buffers(),
             *slots(F32, (T, NB), (T, NB), (T, D)),
             pltpu.VMEM((T, D), BF16),
             *tile_semaphores(),
             DMA((TWO, TWO)),
-            DMA((PARTS,)),
+            DMA((TWO, TWO)),
+            *scatter_scratch(),
         ],
         cost_estimate=pl.CostEstimate(flops=12 * T * D * FF, bytes_accessed=mib(200), transcendentals=T * FF),
-        compiler_params=PARAMS(vmem_limit_bytes=mib(62)),
+        compiler_params=PARAMS(collective_id=0, has_side_effects=True, vmem_limit_bytes=mib(63)),
         name="layer0",
     )(*args)
-
-
-def reduce_scatter(*grads):
-    return pl.pallas_call(
-        scatter_kernel,
-        out_shape=(*shaped(BF16, (GROUP, PACKED, LANES)), *shaped(F32, (LAYERS, ROWS, D), (8, HALF))),
-        in_specs=[ANY] * 2,
-        out_specs=(VMEM,) * 3,
-        scratch_shapes=scatter_scratch(),
-        compiler_params=PARAMS(collective_id=0, has_side_effects=True, vmem_limit_bytes=mib(60)),
-        name="reduce_scatter",
-    )(*grads)
 
 
 def adamw(w, m, v, g):
@@ -1012,15 +1036,14 @@
 
 
 def terms(x, dy, weights):
-    g, u, act0, h, a0t, a1, a1t = forward(x, *weights)
+    by_gate, by_up, act0, h, scale, a0t, a1, a1t = forward(x, *weights)
     grad1, _act1, dg, du = layer1(a1, a1t, dy, *weights)
-    return grad1, layer0(a0t, h, dy, *weights, g, u, act0, dg, du)
+    return (grad1, *layer0(a0t, h, scale, dy, *weights, by_gate, by_up, act0, dg, du, grad1))
 
 
 def local_step(x, dy, *arrays):
     weights, m, v = (arrays[i : i + PARTS] for i in range(0, len(arrays), PARTS))
-    grad1, grad0 = terms(x[0], dy[0], weights)
-    sums = reduce_scatter(grad0, grad1)
+    sums = terms(x[0], dy[0], weights)[-3:]
     send, down, *new = optimizer(sums, weights, turned(m), turned(v))
     spaces = (pltpu.VMEM, pltpu.VMEM, pltpu.VMEM, pltpu.HBM)
     gathered = all_gather(send, down)

time: 512 us -> 451 us (0.88)
  Pallas kernels: 510 us -> 449 us
    pallas_call x2 -> x1, Pallas kernels: 237 us -> 176 us  [layer0(): pl.pallas_call(layer0_kernel, out_shape=(*shaped(BF16, GRAD, (GROUP, PACK...]
where the time goes in v2:
time: 451 us; the launch traced here: 450 us
  Pallas kernels  449 us (100%)
    pallas_call x1, Pallas kernels, layer0(): pl.pallas_call(layer0_kernel, out_shape=(*shaped(BF16, GRAD, (GROUP, PACK...  176 us
    pallas_call x1, Pallas kernels, all_gather(): pl.pallas_call(gather_kernel, out_shape=(pltpu.VMEM((LAYERS, len(PAIR), R...  127 us
    pallas_call x1, Pallas kernels, layer1(): pl.pallas_call(layer1_kernel, out_shape=shaped(BF16, GRAD, (T, FF), (T, F...  74.8 us
    pallas_call x1, Pallas kernels, forward(): pl.pallas_call(forward_kernel, out_shape=(*shaped(F32, (T, FF), (T, FF)),...  46.8 us
    pallas_call x1, Pallas kernels, put(): pl.pallas_call(put_kernel, out_shape=(wide_shape, wide_shape, jax.ShapeDt...  18.5 us

profile of v2, /device:TPU:1, one launch (start us, length us, event | category | flops | bytes accessed | tf_op | source)
XLA Modules:
  0.0 449.9 jit_solution(12273870489767593270)
XLA Ops:
  0.6 46.8 %forward.1 = (f32[1024,6144]{1,0:T(8,128)}, f32[1024,6144]{1,0:T(8,128)}, bf16[1024,6144]{1,0:T(8,128)(2,1)}, bf16[1024,768]{1,0:T(8,128)(2,1)}, f32[1024,128]{1...) custom-call(bf16[1024,768]{1,0:T(8,128)(2,1)} %bitcast.20, ...), custom_call_target="tpu_custom_call" | custom-call | flops 28991029248 | bytes 104857600 | tf_op jit(solution)/shard_map/forward/pallas_call | solution.py:650
  47.5 74.8 %layer1.1 = (bf16[6,3,2,4,4,4,48,128]{7,6,5,4,3,2,1,0:T(8,128)(2,1)}, bf16[1024,6144]{1,0:T(8,128)(2,1)}, bf16[1024,6144]{1,0:T(8,128)(2,1)}, bf16[1024,6144]{1,0:T(8,128)(2,1)}) custom-call(bf16[1024,768]{1,0:T(8,128)(2,1)} %get-tuple-element.44.a1_ref, bf16[768,1024]{1,0:T(8,128)(2,1)} %get-tuple-element.45.a1t_ref, bf16[1024,768]{1,0:T(8,128)(2,1)} %bitcast.21, ...), custom_call_target="tpu_custom_call" | custom-call | flops 57982058496 | bytes 125829120 | tf_op jit(solution)/shard_map/layer1/pallas_call | solution.py:936
  122.3 175.8 %layer0.1 = (bf16[6,3,2,4,4,4,48,128]{7,6,5,4,3,2,1,0:T(8,128)(2,1)}, bf16[8,80,256]{2,1,0:T(8,128)(2,1)}, f32[2,48,768]{2,1,0:T(8,128)}, f32[8,128]{1,0:T(8,128)}) custom-call(bf16[768,1024]{1,0:T(8,128)(2,1)} %get-tuple-element.38.a0t_ref, bf16[1024,768]{1,0:T(8,128)(2,1)} %get-tuple-element.39.h_ref, f32[1024,128]{1,0:T(8,128)} %get-tuple-element.40.scale_ref, ...), custom_call_target="tpu_custom_call" | custom-call | flops 57982058496 | bytes 209715200 | tf_op jit(solution)/shard_map/layer0/pallas_call | solution.py:949
  298.0 5.9 %optimizer.1 = (bf16[8,80,256]{2,1,0:T(8,128)(2,1)}, bf16[2,48,768]{2,1,0:T(8,128)(2,1)}, f32[6,2,6144]{2,1,0:T(2,128)}, f32[6,2,6144]{2,1,0:T(2,128)}, f32[2,48...) custom-call(bf16[8,80,256]{2,1,0:T(8,128)(2,1)} %get-tuple-element.49.take_ref, ...), custom_call_target="tpu_custom_call" | custom-call | tf_op jit(solution)/shard_map/optimizer/pallas_call | solution.py:1016
  303.9 127.3 %all_gather.1 = (bf16[2,2,4,4,48,6144]{5,4,3,2,1,0:T(8,128)(2,1)S(1)}, bf16[4,4,4,2,48,768]{5,4,3,2,1,0:T(8,128)(2,1)S(1)}, bf16[4,4,4,2,48,512]{5,4,3,2,1,0:T(8,128)(2,1)S(1)}, bf16[4,4,4,2,48,256]{5,4,3,2,1,0:T(8,128)(2,1)}) custom-call(bf16[8,80,256]{2,1,0:T(8,128)(2,1)} %get-tuple-element.52.rows_ref, bf16[2,48,768]{2,1,0:T(8,128)(2,1)} %get-tuple-element.53.down_ref), custom_call_target="tpu_custom_call" | custom-call | tf_op jit(solution)/shard_map/all_gather/pallas_call | solution.py:494
  431.2 18.5 %put.1 = (bf16[2,4,4,48,6144]{4,3,2,1,0:T(8,128)(2,1)}, bf16[2,4,4,48,6144]{4,3,2,1,0:T(8,128)(2,1)}, bf16[2,4,4,4,2,48,768]{6,5,4,3,2,1,0:T(8,128)(2,1)}) custom-call(bf16[2,2,4,4,48,6144]{5,4,3,2,1,0:T(8,128)(2,1)S(1)} %get-tuple-element.54.wide_ref, bf16[4,4,4,2,48,768]{5,4,3,2,1,0:T(8,128)(2,1)S(1)} %get-tuple-element.55.down0_ref, ...), custom_call_target="tpu_custom_call" | custom-call | tf_op jit(solution)/shard_map/put/pallas_call | solution.py:535

commit v3 on v2

--- a/solution.py
+++ b/solution.py
@@ -135,12 +135,9 @@
 EACH = UNITS // LAYERS
 AHEAD = len(PAIR)
 SIDES = ((0, 1), (1, -1))
+REACH = (*SIDES, (2, 2))
 PASSED, DIRECT = 1, 0
 CELL = (ROWS, HALF)
-
-
-def tile(half):
-    return pl.ds(16 * half, 16 + 16 * half)
 
 
 def pair_of(half):
@@ -153,73 +150,72 @@
         self.axis, self.cut = (k + stage) % PARTS, (k - 1) % PARTS
         self.last = self.axis == self.cut
         self.coords, self.core = coords, core
-        self.data, self.ra, self.rb = bufs
+        self.data, self.ra, *self.rb = bufs
         self.ss, self.rs, self.credit = ss, rs, credit
         self.i = coords[self.axis]
 
     def to(self, by):
         return device(moved(self.coords, self.axis, by), self.core)
 
-    def index(self, place, half):
-        at = [place if a == self.axis else pair_of(half) if a == self.cut else ALL for a in self.axes]
-        return (*at, tile(half) if self.last else ALL, ALL)
-
-    def landing(self, half):
-        return (tile(half), ALL) if self.last else ()
+    def index(self, by, half):
+        place = around(self.i + by)
+        return (*(place if a == self.axis else pair_of(half) if a == self.cut else ALL for a in self.axes), ALL, ALL)
 
     def out(self, half):
-        return self.landing(half) or (*(pair_of(half) if a == self.cut else ALL for a in self.axes if a != self.axis), ALL, ALL)
+        return (*(pair_of(half) if a == self.cut else ALL for a in self.axes if a != self.axis), ALL, ALL)
+
+    def copy(self, n, src, dst, by):
+        return remote(src, dst, self.ss.at[n], self.rs.at[n], self.to(by))
 
     def firsts(self):
+        if self.last:
+            return {n: self.copy(n, self.data.at[self.index(by, 0)], self.ra.at[n], by) for n, by in REACH}
         out = {}
         for side, by in SIDES:
             for which, step, half in ((PASSED, by + by, 1 - side), (DIRECT, by, side)):
-                at = self.index(around(self.i + step), half)
-                n = len(out)
-                out[side, which] = remote(self.data.at[at], self.ra.at[(side, which) + self.landing(half)], self.ss.at[n], self.rs.at[n], self.to(by))
+                out[side, which] = self.copy(len(out), self.data.at[self.index(step, half)], self.ra.at[side, which], by)
         return out
 
     def seconds(self):
-        out = []
-        for side, by in SIDES:
-            at, n = self.landing(1 - side), len(SIDES) * len(PAIR) + side
-            out.append(remote(self.ra.at[(side, PASSED) + at], self.rb.at[(side,) + at], self.ss.at[n], self.rs.at[n], self.to(by)))
-        return out
+        return [self.copy(len(SIDES) * len(PAIR) + side, self.ra.at[side, PASSED], self.rb[0].at[side], by) for side, by in SIDES]
+
+    def peers(self):
+        return REACH if self.last else SIDES
 
     def start(self, again):
         @pl.when(again)
         def _():
-            for side, _by in SIDES:
-                pl.semaphore_wait(self.credit.at[side], 1)
+            for n, _by in self.peers():
+                pl.semaphore_wait(self.credit.at[n], 1)
 
         begin(self.firsts().values())
 
     def middle(self):
         copies = self.firsts()
         for side, by in SIDES:
-            half = 1 - side
-            at = (side, PASSED) + self.landing(half)
             copies[side, PASSED].wait_recv()
-            here = self.data[self.index(around(self.i + by), half)].astype(F32)
-            self.ra[at] = (here + self.ra[at].astype(F32)).astype(BF16)
+            here = self.data[self.index(by, 1 - side)].astype(F32)
+            self.ra[side, PASSED] = (here + self.ra[side, PASSED].astype(F32)).astype(BF16)
         begin(self.seconds())
 
     def finish(self, store, more):
-        copies, passed = self.firsts(), self.seconds()
-        for side, _by in SIDES:
-            copies[side, DIRECT].wait_recv()
-            passed[side].wait_recv()
-        for half in PAIR:
-            here = self.data[self.index(self.i, half)].astype(F32)
-            near = self.ra[(half, DIRECT) + self.landing(half)].astype(F32)
-            far = self.rb[(1 - half,) + self.landing(half)].astype(F32)
-            store(self.out(half), here + near + far)
+        copies = self.firsts()
+        passed = [] if self.last else self.seconds()
+        if self.last:
+            received(copies.values())
+            store((ALL, ALL), sum(self.ra[n].astype(F32) for n, _by in REACH) + self.data[self.index(0, 0)].astype(F32))
+        else:
+            received([copies[side, DIRECT] for side, _by in SIDES])
+            received(passed)
+            for half in PAIR:
+                here = self.data[self.index(0, half)].astype(F32)
+                store(self.out(half), here + self.ra[half, DIRECT].astype(F32) + self.rb[0][1 - half].astype(F32))
         sent([*copies.values(), *passed])
 
         @pl.when(more)
         def _():
-            for side, by in SIDES:
-                signal(self.credit.at[side], self.to(-by))
+            for n, by in self.peers():
+                signal(self.credit.at[n], self.to(-by))
 
 
 def axes_left(k, stage):
@@ -252,17 +248,22 @@
             for k in range(PARTS)
         ]
 
-    def feed(self, u):
-        @pl.when(u >= AHEAD)
-        def _():
-            pl.semaphore_wait(self.s_credit, 1)
-
+    def start(self, u, copy):
         for layer, its in ((1, u < EACH), (0, u >= EACH)):
 
             @pl.when(its)
             def _(layer=layer):
-                for k in range(PARTS):
-                    begin([self.swap(u, k, layer), self.load(u, k, layer)])
+                begin([copy(u, k, layer) for k in range(PARTS)])
+
+    def start_swap(self, u):
+        @pl.when(u >= AHEAD)
+        def _():
+            pl.semaphore_wait(self.s_credit, 1)
+
+        self.start(u, self.swap)
+
+    def start_load(self, u):
+        self.start(u, self.load)
 
     def add(self, u):
         for k in range(PARTS):
@@ -284,8 +285,8 @@
         for ring in self.rings(u, 0):
             ring.start(u >= AHEAD)
 
-    def at_stages(self, i, step):
-        for stage in AXES:
+    def at_stages(self, i, stages, step):
+        for stage in reversed(stages):
             u = i - stage
 
             @pl.when((u >= 0) & (u < UNITS))
@@ -297,7 +298,7 @@
             for ring in self.rings(u, stage):
                 ring.middle()
 
-        self.at_stages(i, step)
+        self.at_stages(i, AXES[:-1], step)
 
     def finishes(self, i):
         def step(u, stage):
@@ -308,7 +309,7 @@
                 for ring in self.rings(u, stage + 1):
                     ring.start(u >= AHEAD)
 
-        self.at_stages(i, step)
+        self.at_stages(i, AXES, step)
 
     def into(self, u, k, ring, stage):
         def store(at, value):
@@ -338,11 +339,13 @@
             left = [len(PAIR) if a == (k - 1) % PARTS else RING for a in axes_left(k, stage + 1)]
             if left:
                 out.append(pltpu.VMEM((*two, *(RING for _ in left), *CELL), BF16))
-            out.append(pltpu.VMEM((*two, *two, *two, *left, *CELL), BF16))
-            out.append(pltpu.VMEM((*two, *two, *left, *CELL), BF16))
+                out.append(pltpu.VMEM((*two, *two, *two, *left, *CELL), BF16))
+                out.append(pltpu.VMEM((*two, *two, *left, *CELL), BF16))
+            else:
+                out.append(pltpu.VMEM((*two, len(REACH), *CELL), BF16))
     each = (*two, PARTS)
     out += [pltpu.VMEM((UNITS, PARTS, *CELL), BF16), pltpu.VMEM((8, HALF), F32)]
-    out += [DMA(each)] * PARTS + [DMA((*each, PARTS, 6))] * len(PAIR) + [SIGNALS((PARTS, PARTS, *two)), SIGNALS]
+    out += [DMA(each)] * PARTS + [DMA((*each, PARTS, 6))] * len(PAIR) + [SIGNALS((PARTS, PARTS, len(REACH))), SIGNALS]
     out += [pltpu.VMEM((PACKED, LANES), F32), pltpu.VMEM((GROUP, PACKED, LANES), BF16), pltpu.VMEM((GROUP, PACKED, LANES), BF16)]
     out += [pltpu.VMEM((PLANE, *two, 8, HALF), F32)]
     return out + [DMA((GROUP,))] * 4 + [DMA((PLANE,))] * 2
@@ -356,9 +359,11 @@
     for stage in AXES:
         row, after = [], []
         for k in range(PARTS):
+            own = [data[k]]
             if axes_left(k, stage + 1):
                 after.append(next(scratch))
-            row.append((data[k], next(scratch), next(scratch)))
+                own.append(next(scratch))
+            row.append((*own, next(scratch)))
         stages.append(row)
         data = after
     blocks, squares, *rest = scratch
@@ -413,7 +418,6 @@
     for n, (where, c) in enumerate(group_peers(coords, core)):
         swaps.append(remote(rows_ref.at[CORES * where[-1] + c], take.at[me], t_send.at[n], t_recv.at[n], device(where, c)))
     begin(swaps)
-    take[me] = rows_ref[me]
     here = (*coords, core)
     own = pltpu.make_async_copy(down_ref.at[1, :, lanes(PARTS - 1, LANES)], last_out.at[here], own_sem)
     own.start()
@@ -432,18 +436,19 @@
             base += spot[-1] * LANES
         return wide_out.at[(layer, which, *at[:-1], ALL, pl.ds(pl.multiple_of(base, many * LANES), many * LANES))]
 
-    received(swaps)
-    for j in range(GROUP):
-        rows = take[j].astype(F32)
-        for q in range(len(stage)):
-            stage[q, pl.ds(OWN * j, OWN), :] = rows[OWN * q : OWN * q + OWN]
-    for layer in PAIR:
-        for which in (GATE, UP):
-            for k in range(PARTS):
-                at = pl.multiple_of((GROUP * k + RING * core + z) * LANES, LANES)
-                wide_out[layer, which, x, y, :, pl.ds(at, LANES)] = stage[packed_row(layer, which, k) // OWN].astype(BF16)
-    sent(swaps)
-    own.wait()
+    def unpack():
+        take[me] = rows_ref[me]
+        received(swaps)
+        for j in range(GROUP):
+            rows = take[j].astype(F32)
+            for q in range(len(stage)):
+                stage[q, pl.ds(OWN * j, OWN), :] = rows[OWN * q : OWN * q + OWN]
+        for layer in PAIR:
+            for which in (GATE, UP):
+                for k in range(PARTS):
+                    at = pl.multiple_of((GROUP * k + RING * core + z) * LANES, LANES)
+                    wide_out[layer, which, x, y, :, pl.ds(at, LANES)] = stage[packed_row(layer, which, k) // OWN].astype(BF16)
+        sent(swaps)
 
     def spot(k, turn, by):
         out = []
@@ -459,33 +464,54 @@
         shares.append(remote(ref, ref, c_send.at[k, turn, which, n], c_recv.at[k, turn, which, n], partner))
         shares[-1].start()
 
-    everything = [(which, k, side, by) for which in (GATE, UP, DOWN) for k in range(PARTS) for side, by in SIDES]
-    for turn in AXES:
-
-        def copy(which, k, by, n, layer, start):
-            ref = piece(which, k, layer, spot(k, turn, start))
-            sems = send.at[k, turn, which, n], recv.at[k, turn, which, n]
-            return remote(ref, ref, *sems, device(moved(coords, (k - 1 - turn) % PARTS, by), core))
-
-        first = [copy(which, k, by, side, side, 0) for which, k, side, by in everything]
-        other = [copy(which, k, by, 2 + side, 1 - side, 0) for which, k, side, by in everything]
-        far = [copy(which, k, by, 4 + side, side, -by) for which, k, side, by in everything]
-        begin(first)
-        begin(other)
-        if turn == 0:
-            for which, k, side, by in everything:
-                share(which, k, side, turn, 0, side)
-        for n, (which, k, side, by) in enumerate(everything):
-            first[n].wait_recv()
-            far[n].start()
-            share(which, k, side, turn, -by, 2 + side)
-        for n, (which, k, side, by) in enumerate(everything):
-            other[n].wait_recv()
-            share(which, k, 1 - side, turn, -by, 4 + side)
-        for n, (which, k, side, by) in enumerate(everything):
-            far[n].wait_recv()
-            share(which, k, side, turn, 2, 6 + side)
-        sent(first + other + far)
+    class Turn:
+        def __init__(self, matrices, turn):
+            self.turn = turn
+            self.all = [(which, k, side, by) for which in matrices for k in range(PARTS) for side, by in SIDES]
+            self.first = [self.copy(which, k, by, side, side, 0) for which, k, side, by in self.all]
+            self.other = [self.copy(which, k, by, 2 + side, 1 - side, 0) for which, k, side, by in self.all]
+            self.far = [self.copy(which, k, by, 4 + side, side, -by) for which, k, side, by in self.all]
+
+        def copy(self, which, k, by, n, layer, start):
+            ref = piece(which, k, layer, spot(k, self.turn, start))
+            sems = send.at[k, self.turn, which, n], recv.at[k, self.turn, which, n]
+            return remote(ref, ref, *sems, device(moved(coords, (k - 1 - self.turn) % PARTS, by), core))
+
+        def start(self):
+            begin(self.first)
+            begin(self.other)
+            if self.turn == 0:
+                for which, k, side, by in self.all:
+                    share(which, k, side, self.turn, 0, side)
+
+        def near(self):
+            for n, (which, k, side, by) in enumerate(self.all):
+                self.first[n].wait_recv()
+                self.far[n].start()
+                share(which, k, side, self.turn, -by, 2 + side)
+            for n, (which, k, side, by) in enumerate(self.all):
+                self.other[n].wait_recv()
+                share(which, k, 1 - side, self.turn, -by, 4 + side)
+
+        def done(self):
+            for n, (which, k, side, by) in enumerate(self.all):
+                self.far[n].wait_recv()
+                share(which, k, side, self.turn, 2, 6 + side)
+            sent(self.first + self.other + self.far)
+
+    streams = [[Turn(matrices, turn) for matrices in ((DOWN,), (GATE, UP))] for turn in AXES]
+    own.wait()
+    for downs, wides in streams:
+        if downs.turn == 0:
+            downs.start()
+            unpack()
+            wides.start()
+        downs.near()
+        wides.near()
+        for stream, now in enumerate((downs, wides)):
+            now.done()
+            if now.turn + 1 < len(streams):
+                streams[now.turn + 1][stream].start()
     end(shares)
 
 
@@ -785,9 +811,11 @@
 FIRST_WIDE = FIRST_DOWN + TILES
 LAST_STEPS = FIRST_WIDE + N_J
 STEPS = LAST_STEPS + 6
-MIDDLES = (3, 7, 11, 17, 20, 22, 25, 28, 31, *range(LAST_STEPS + 1, STEPS))
-FINISHES = (5, 9, 13, 19, 21, 23, 26, 29, *range(LAST_STEPS, STEPS))
-FEEDS = (5, 9, 13, 19, 21, 23, 27, 29, LAST_STEPS, LAST_STEPS + 1)
+MIDDLES = (4, 8, 11, 15, 21, 23, 25, 27, 30, *range(LAST_STEPS + 1, STEPS - 1))
+ADDS = (2, 3, 8, 11, 14, 21, 23, 25, 28, 29, LAST_STEPS + 1, LAST_STEPS + 2)
+FINISHES = (7, 10, 13, 20, 22, 24, 26, 28, *range(LAST_STEPS, STEPS))
+LOADS = FINISHES[: UNITS - AHEAD]
+SWAPS = (2, 3, 8, 11, 19, 21, 26, 27, LAST_STEPS - 1, LAST_STEPS)
 
 
 def due(step, steps, do):
@@ -848,10 +876,6 @@
         end(weights(j))
         end(products(j))
 
-        @pl.when(j >= AHEAD)
-        def _():
-            end(outs(j - AHEAD))
-
         @pl.when(j + 1 < N_J)
         def _():
             begin(weights(j + 1))
@@ -862,6 +886,11 @@
             terms[s, GATE, rows, :] = (d * gate[s, rows, :]).astype(BF16)
             terms[s, UP, rows, :] = (d * up[s, rows, :]).astype(BF16)
         wide_terms(a0t_ref, terms, (out_g, out_u), s)
+
+        @pl.when(j >= 1)
+        def _():
+            end(outs(j - 1))
+
         begin(outs(j))
 
     begin(da_in(0))
@@ -869,10 +898,10 @@
     begin(products(0))
     enter(sc.coords, sc.core)
     sc.squares[:] = jnp.zeros_like(sc.squares)
-    sc.feed(0)
-    sc.feed(1)
+    for u in range(AHEAD):
+        sc.start_swap(u)
+        sc.start_load(u)
     total[:] = jnp.zeros_like(total)
-    sc.add(0)
 
     @loop(STEPS)
     def _(step):
@@ -899,19 +928,13 @@
 
         @pl.when(step == LAST_STEPS - 1)
         def _():
-            for j in PAIR:
-                end(outs(N_J - AHEAD + j))
-
-        def middles_and_add(i):
-            sc.middles(i)
-
-            @pl.when(i + 1 < UNITS)
-            def _():
-                sc.add(i + 1)
-
-        due(step, MIDDLES, middles_and_add)
+            end(outs(N_J - 1))
+
+        due(step, MIDDLES, sc.middles)
+        due(step, ADDS, sc.add)
         due(step, FINISHES, sc.finishes)
-        due(step, FEEDS, lambda n: sc.feed(n + AHEAD))
+        due(step, LOADS, lambda n: sc.start_load(n + AHEAD))
+        due(step, SWAPS, lambda n: sc.start_swap(n + AHEAD))
 
     last_swap(sc, take_ref, own_ref, ss_ref, *rest)
 

time: 451 us -> 443 us (0.982)
  Pallas kernels: 449 us -> 441 us
    pallas_call x1, Pallas kernels: 176 us -> 171 us  [layer0(): pl.pallas_call(layer0_kernel, out_shape=(*shaped(BF16, GRAD, (GROUP, PACK...]
where the time goes in v3:
time: 443 us; the launch traced here: 442 us
  Pallas kernels  441 us (100%)
    pallas_call x1, Pallas kernels, layer0(): pl.pallas_call(layer0_kernel, out_shape=(*shaped(BF16, GRAD, (GROUP, PACK...  171 us
    pallas_call x1, Pallas kernels, all_gather(): pl.pallas_call(gather_kernel, out_shape=(pltpu.VMEM((LAYERS, len(PAIR), R...  124 us
    pallas_call x1, Pallas kernels, layer1(): pl.pallas_call(layer1_kernel, out_shape=shaped(BF16, GRAD, (T, FF), (T, F...  74.8 us
    pallas_call x1, Pallas kernels, forward(): pl.pallas_call(forward_kernel, out_shape=(*shaped(F32, (T, FF), (T, FF)),...  46.8 us
    pallas_call x1, Pallas kernels, put(): pl.pallas_call(put_kernel, out_shape=(wide_shape, wide_shape, jax.ShapeDt...  18.5 us

profile of v3, /device:TPU:1, one launch (start us, length us, event | category | flops | bytes accessed | tf_op | source)
XLA Modules:
  0.0 441.9 jit_solution(12920070944640252445)
XLA Ops:
  0.6 46.8 %forward.1 = (f32[1024,6144]{1,0:T(8,128)}, f32[1024,6144]{1,0:T(8,128)}, bf16[1024,6144]{1,0:T(8,128)(2,1)}, bf16[1024,768]{1,0:T(8,128)(2,1)}, f32[1024,128]{1...) custom-call(bf16[1024,768]{1,0:T(8,128)(2,1)} %bitcast.20, ...), custom_call_target="tpu_custom_call" | custom-call | flops 28991029248 | bytes 104857600 | tf_op jit(solution)/shard_map/forward/pallas_call | solution.py:676
  47.5 74.8 %layer1.1 = (bf16[6,3,2,4,4,4,48,128]{7,6,5,4,3,2,1,0:T(8,128)(2,1)}, bf16[1024,6144]{1,0:T(8,128)(2,1)}, bf16[1024,6144]{1,0:T(8,128)(2,1)}, bf16[1024,6144]{1,0:T(8,128)(2,1)}) custom-call(bf16[1024,768]{1,0:T(8,128)(2,1)} %get-tuple-element.44.a1_ref, bf16[768,1024]{1,0:T(8,128)(2,1)} %get-tuple-element.45.a1t_ref, bf16[1024,768]{1,0:T(8,128)(2,1)} %bitcast.21, ...), custom_call_target="tpu_custom_call" | custom-call | flops 57982058496 | bytes 125829120 | tf_op jit(solution)/shard_map/layer1/pallas_call | solution.py:959
  122.3 170.6 %layer0.1 = (bf16[6,3,2,4,4,4,48,128]{7,6,5,4,3,2,1,0:T(8,128)(2,1)}, bf16[8,80,256]{2,1,0:T(8,128)(2,1)}, f32[2,48,768]{2,1,0:T(8,128)}, f32[8,128]{1,0:T(8,128)}) custom-call(bf16[768,1024]{1,0:T(8,128)(2,1)} %get-tuple-element.38.a0t_ref, bf16[1024,768]{1,0:T(8,128)(2,1)} %get-tuple-element.39.h_ref, f32[1024,128]{1,0:T(8,128)} %get-tuple-element.40.scale_ref, ...), custom_call_target="tpu_custom_call" | custom-call | flops 57982058496 | bytes 209715200 | tf_op jit(solution)/shard_map/layer0/pallas_call | solution.py:972
  292.9 5.9 %optimizer.1 = (bf16[8,80,256]{2,1,0:T(8,128)(2,1)}, bf16[2,48,768]{2,1,0:T(8,128)(2,1)}, f32[6,2,6144]{2,1,0:T(2,128)}, f32[6,2,6144]{2,1,0:T(2,128)}, f32[2,48...) custom-call(bf16[8,80,256]{2,1,0:T(8,128)(2,1)} %get-tuple-element.49.take_ref, ...), custom_call_target="tpu_custom_call" | custom-call | tf_op jit(solution)/shard_map/optimizer/pallas_call | solution.py:1039
  298.8 124.4 %all_gather.1 = (bf16[2,2,4,4,48,6144]{5,4,3,2,1,0:T(8,128)(2,1)S(1)}, bf16[4,4,4,2,48,768]{5,4,3,2,1,0:T(8,128)(2,1)S(1)}, bf16[4,4,4,2,48,512]{5,4,3,2,1,0:T(8,128)(2,1)S(1)}, bf16[4,4,4,2,48,256]{5,4,3,2,1,0:T(8,128)(2,1)}) custom-call(bf16[8,80,256]{2,1,0:T(8,128)(2,1)} %get-tuple-element.52.rows_ref, bf16[2,48,768]{2,1,0:T(8,128)(2,1)} %get-tuple-element.53.down_ref), custom_call_target="tpu_custom_call" | custom-call | tf_op jit(solution)/shard_map/all_gather/pallas_call | solution.py:520
  423.2 18.5 %put.1 = (bf16[2,4,4,48,6144]{4,3,2,1,0:T(8,128)(2,1)}, bf16[2,4,4,48,6144]{4,3,2,1,0:T(8,128)(2,1)}, bf16[2,4,4,4,2,48,768]{6,5,4,3,2,1,0:T(8,128)(2,1)}) custom-call(bf16[2,2,4,4,48,6144]{5,4,3,2,1,0:T(8,128)(2,1)S(1)} %get-tuple-element.54.wide_ref, bf16[4,4,4,2,48,768]{5,4,3,2,1,0:T(8,128)(2,1)S(1)} %get-tuple-element.55.down0_ref, ...), custom_call_target="tpu_custom_call" | custom-call | tf_op jit(solution)/shard_map/put/pallas_call | solution.py:561

commit v4 on v3

--- a/solution.py
+++ b/solution.py
@@ -125,7 +125,7 @@
     pl.semaphore_wait(barrier, len(peers))
 
 
-GATE, UP, DOWN = range(3)
+GATE, UP, DOWN, WIDE = range(4)
 ORDER = [(1, which, half) for half in PAIR for which in (GATE, UP)]
 ORDER += [(layer, DOWN, half) for layer in (1, 0) for half in PAIR]
 ORDER += [(0, which, half) for half in PAIR for which in (GATE, UP)]
@@ -430,11 +430,12 @@
             if layer and k == PARTS - 1:
                 return last_out.at[(*at, core)]
             return (down0_out, down1_out)[layer].at[(*at, core, ALL, lanes(k, LANES))]
+        matrix = ALL if which == WIDE else which
         base = (k * GROUP + core * RING) * LANES
         many = RING if spot[-1] is None else 1
         if many == 1:
             base += spot[-1] * LANES
-        return wide_out.at[(layer, which, *at[:-1], ALL, pl.ds(pl.multiple_of(base, many * LANES), many * LANES))]
+        return wide_out.at[(layer, matrix, *at[:-1], ALL, pl.ds(pl.multiple_of(base, many * LANES), many * LANES))]
 
     def unpack():
         take[me] = rows_ref[me]
@@ -461,7 +462,7 @@
 
     def share(which, k, layer, turn, by, n):
         ref = piece(which, k, layer, spot(k, turn, by))
-        shares.append(remote(ref, ref, c_send.at[k, turn, which, n], c_recv.at[k, turn, which, n], partner))
+        shares.append(remote(ref, ref, c_send.at[k, turn, which % PARTS, n], c_recv.at[k, turn, which % PARTS, n], partner))
         shares[-1].start()
 
     class Turn:
@@ -474,7 +475,7 @@
 
         def copy(self, which, k, by, n, layer, start):
             ref = piece(which, k, layer, spot(k, self.turn, start))
-            sems = send.at[k, self.turn, which, n], recv.at[k, self.turn, which, n]
+            sems = send.at[k, self.turn, which % PARTS, n], recv.at[k, self.turn, which % PARTS, n]
             return remote(ref, ref, *sems, device(moved(coords, (k - 1 - self.turn) % PARTS, by), core))
 
         def start(self):
@@ -499,7 +500,7 @@
                 share(which, k, side, self.turn, 2, 6 + side)
             sent(self.first + self.other + self.far)
 
-    streams = [[Turn(matrices, turn) for matrices in ((DOWN,), (GATE, UP))] for turn in AXES]
+    streams = [[Turn(matrices, turn) for matrices in ((DOWN,), (WIDE,) if turn < AXES[-1] else (GATE, UP))] for turn in AXES]
     own.wait()
     for downs, wides in streams:
         if downs.turn == 0:
@@ -599,8 +600,8 @@
     return u * (sig + silu * (1 - sig)), silu, (silu * u).astype(BF16)
 
 
-def forward_kernel(x_ref, wg_ref, wu_ref, wd_ref, g_ref, u_ref, act_ref, h_ref, scale_ref, a0t_ref, a1_ref, a1t_ref,
-                   a0, wg, wu, wd, gate, up, act, w_sem, d_sem, g_sem, a_sem):
+def forward_part(x_ref, wg_ref, wu_ref, wd_ref, g_ref, u_ref, act_ref, h_ref, scale_ref, a0t_ref, a1_ref, a1t_ref,
+                 a0, wg, wu, wd, gate, up, act, w_sem, d_sem, g_sem, a_sem, meanwhile):
     def weights(j):
         s = slot(j)
         return [pltpu.make_async_copy(ref.at[0, :, columns(j)], buf.at[s], w_sem.at[n, s]) for n, (ref, buf) in enumerate(((wg_ref, wg), (wu_ref, wu)))]
@@ -658,6 +659,7 @@
             y = nn(act[rows, :], wd[slot(n)]).astype(BF16)
             h_ref[rows, columns(n, LANES)] = x_ref[rows, columns(n, LANES)] + y
 
+    meanwhile()
     norm(h_ref, a1_ref, a1t_ref)
     for j in PAIR:
         end(stores(N_J - AHEAD + j))
@@ -669,29 +671,6 @@
 
 def slots(dtype, *shapes):
     return [pltpu.VMEM((len(PAIR), *s), dtype) for s in shapes]
-
-
-def forward(x, *weights):
-    two = len(PAIR)
-    return pl.pallas_call(
-        forward_kernel,
-        out_shape=(*shaped(F32, (T, FF), (T, FF)), *shaped(BF16, (T, FF), (T, D)), *shaped(F32, (T, HALF)), *shaped(BF16, (D, T), (T, D), (D, T))),
-        in_specs=[VMEM, ANY, ANY, ANY],
-        out_specs=(ANY,) * 3 + (VMEM,) * 5,
-        scratch_shapes=[
-            pltpu.VMEM((T, D), BF16),
-            *slots(BF16, (D, NB), (D, NB), (FF, LANES)),
-            *slots(F32, (T, NB), (T, NB)),
-            pltpu.VMEM((T, FF), BF16),
-            DMA((two, two)),
-            DMA((two,)),
-            DMA((two, two)),
-            DMA((two,)),
-        ],
-        cost_estimate=pl.CostEstimate(flops=6 * T * D * FF, bytes_accessed=mib(100), transcendentals=T * FF),
-        compiler_params=PARAMS(vmem_limit_bytes=mib(62)),
-        name="forward",
-    )(x, *weights)
 
 
 def both_of(a, b):
@@ -762,7 +741,8 @@
     return comes, step, finish
 
 
-def layer1_kernel(a1_ref, a1t_ref, dy_ref, wg_ref, wu_ref, wd_ref, grad_ref, act1_ref, dg_ref, du_ref,
+def layer1_kernel(x_ref, dy_ref, wg_ref, wu_ref, wd_ref, g_ref, u_ref, act0_ref, h_ref, scale_ref, a0t_ref, grad_ref, act1_ref, dg_ref, du_ref,
+                  a0, a1_ref, a1t_ref, wide_down, gate, up, act0, f_sem, g_sem, h_sem,
                   wg, wu, wd, act, terms, out_g, out_u, out_d, w_sem, o_sem, d_sem, a_sem, t_sem):
     weights = tiles_of(1, (wg_ref, wu_ref), wd_ref, (wg, wu), wd, w_sem)
     outs = wide_outs(grad_ref, 0, (out_g, out_u), o_sem)
@@ -772,7 +752,8 @@
         pairs = both_of((terms.at[s, GATE], terms.at[s, UP], act.at[s, :, pl.ds(0, NB)]), (dg_ref, du_ref, act1_ref))
         return [pltpu.make_async_copy(src, dst.at[:, columns(j)], t_sem.at[n, s]) for n, (src, dst) in pairs]
 
-    begin(weights(0))
+    forward_part(x_ref, wg_ref, wu_ref, wd_ref, g_ref, u_ref, act0_ref, h_ref, scale_ref, a0t_ref, a1_ref, a1t_ref,
+                 a0, wg, wu, wide_down, gate, up, act0, w_sem, f_sem, g_sem, h_sem, lambda: begin(weights(0)))
 
     @loop(N_J)
     def _(j):
@@ -827,8 +808,9 @@
         do(n)
 
 
-def layer0_kernel(a0t_ref, h_ref, scale_ref, dy_ref, wg_ref, wu_ref, wd_ref, g_ref, u_ref, act0_ref, dg_ref, du_ref, grad1_ref,
+def layer0_kernel(a0t_hbm, h_hbm, scale_hbm, dy_hbm, wg_ref, wu_ref, wd_ref, g_ref, u_ref, act0_ref, dg_ref, du_ref, grad1_ref,
                   grad_ref, take_ref, own_ref, ss_ref,
+                  a0t_ref, h_ref, scale_ref, dy_ref, i_sem,
                   wg, wu, wd, act, terms, out_g, out_u, out_d, gate, up, total, dh,
                   w_sem, o_sem, d_sem, a_sem, l_sem, t_sem, *scratch):
     sc, rest = scatter_of((grad_ref, grad1_ref), scratch)
@@ -893,7 +875,9 @@
 
         begin(outs(j))
 
+    inputs = [pltpu.make_async_copy(src, dst, i_sem.at[n]) for n, (src, dst) in both_of((a0t_hbm, h_hbm, scale_hbm, dy_hbm), (a0t_ref, h_ref, scale_ref, dy_ref))]
     begin(da_in(0))
+    begin(inputs)
     begin(comes(0))
     begin(products(0))
     enter(sc.coords, sc.core)
@@ -912,6 +896,7 @@
         @pl.when(step == FIRST_DOWN - 1)
         def _():
             begin(weights(0))
+            end(inputs)
             states_step()
 
         @pl.when((step >= FIRST_DOWN) & (step < FIRST_WIDE))
@@ -955,26 +940,47 @@
     return [DMA((PARTS, TWO)), DMA((TWO, TWO)), DMA((TWO, TWO)), DMA((TWO,))]
 
 
-def layer1(a1, a1t, dy, *weights):
+def layer1(x, dy, *weights):
     return pl.pallas_call(
         layer1_kernel,
-        out_shape=shaped(BF16, GRAD, (T, FF), (T, FF), (T, FF)),
-        in_specs=[VMEM] * 3 + [ANY] * 3,
-        out_specs=(ANY,) * 4,
-        scratch_shapes=[*tile_buffers(), *tile_semaphores(), DMA((PARTS, TWO))],
-        cost_estimate=pl.CostEstimate(flops=12 * T * D * FF, bytes_accessed=mib(120), transcendentals=T * FF),
-        compiler_params=PARAMS(vmem_limit_bytes=mib(62)),
+        out_shape=(
+            *shaped(F32, (T, FF), (T, FF)),
+            *shaped(BF16, (T, FF), (T, D)),
+            *shaped(F32, (T, HALF)),
+            *shaped(BF16, (D, T), GRAD, (T, FF), (T, FF), (T, FF)),
+        ),
+        in_specs=[VMEM] * 2 + [ANY] * 3,
+        out_specs=(ANY,) * 3 + (VMEM,) * 3 + (ANY,) * 4,
+        scratch_shapes=[
+            *[pltpu.VMEM(s, BF16) for s in ((T, D), (T, D), (D, T))],
+            *slots(BF16, (FF, LANES)),
+            *slots(F32, (T, NB), (T, NB)),
+            pltpu.VMEM((T, FF), BF16),
+            DMA((TWO,)),
+            DMA((TWO, TWO)),
+            DMA((TWO,)),
+            *tile_buffers(),
+            *tile_semaphores(),
+            DMA((PARTS, TWO)),
+        ],
+        cost_estimate=pl.CostEstimate(flops=18 * T * D * FF, bytes_accessed=mib(220), transcendentals=2 * T * FF),
+        compiler_params=PARAMS(vmem_limit_bytes=mib(63)),
         name="layer1",
-    )(a1, a1t, dy, *weights)
+    )(x, dy, *weights)
 
 
 def layer0(*args):
     return pl.pallas_call(
         layer0_kernel,
         out_shape=(*shaped(BF16, GRAD, (GROUP, PACKED, LANES)), *shaped(F32, (LAYERS, ROWS, D), (8, HALF))),
-        in_specs=[VMEM] * 4 + [ANY] * 9,
+        in_specs=[ANY] * 13,
         out_specs=(ANY, VMEM, VMEM, VMEM),
         scratch_shapes=[
+            pltpu.VMEM((D, T), BF16),
+            pltpu.VMEM((T, D), BF16),
+            pltpu.VMEM((T, HALF), F32),
+            pltpu.VMEM((T, D), BF16),
+            DMA((RING,)),
             *tile_buffers(),
             *slots(F32, (T, NB), (T, NB), (T, D)),
             pltpu.VMEM((T, D), BF16),
@@ -1059,8 +1065,7 @@
 
 
 def terms(x, dy, weights):
-    by_gate, by_up, act0, h, scale, a0t, a1, a1t = forward(x, *weights)
-    grad1, _act1, dg, du = layer1(a1, a1t, dy, *weights)
+    by_gate, by_up, act0, h, scale, a0t, grad1, _act1, dg, du = layer1(x, dy, *weights)
     return (grad1, *layer0(a0t, h, scale, dy, *weights, by_gate, by_up, act0, dg, du, grad1))
 
 

time: 443 us -> 438 us (0.989)
  Pallas kernels: 441 us -> 436 us
    pallas_call x2 -> x1, Pallas kernels: 122 us -> 117 us  [layer1(): pl.pallas_call(layer1_kernel, out_shape=(*shaped(F32, (T, FF), (T, FF)),...]
where the time goes in v4:
time: 438 us; the launch traced here: 437 us
  Pallas kernels  436 us (100%)
    pallas_call x1, Pallas kernels, layer0(): pl.pallas_call(layer0_kernel, out_shape=(*shaped(BF16, GRAD, (GROUP, PACK...  170 us
    pallas_call x1, Pallas kernels, all_gather(): pl.pallas_call(gather_kernel, out_shape=(pltpu.VMEM((LAYERS, len(PAIR), R...  125 us
    pallas_call x1, Pallas kernels, layer1(): pl.pallas_call(layer1_kernel, out_shape=(*shaped(F32, (T, FF), (T, FF)),...  117 us
    pallas_call x1, Pallas kernels, put(): pl.pallas_call(put_kernel, out_shape=(wide_shape, wide_shape, jax.ShapeDt...  18.5 us

profile of v4, /device:TPU:1, one launch (start us, length us, event | category | flops | bytes accessed | tf_op | source)
XLA Modules:
  0.0 436.7 jit_solution(5328561036727435532)
XLA Ops:
  0.6 117.3 %layer1.1 = (f32[1024,6144]{1,0:T(8,128)}, f32[1024,6144]{1,0:T(8,128)}, bf16[1024,6144]{1,0:T(8,128)(2,1)}, bf16[1024,768]{1,0:T(8,128)(2,1)}, f32[1024,128]{1,...) custom-call(bf16[1024,768]{1,0:T(8,128)(2,1)} %bitcast.20, ...), custom_call_target="tpu_custom_call" | custom-call | flops 86973087744 | bytes 230686720 | tf_op jit(solution)/shard_map/layer1/pallas_call | solution.py:944
  118.0 169.5 %layer0.1 = (bf16[6,3,2,4,4,4,48,128]{7,6,5,4,3,2,1,0:T(8,128)(2,1)}, bf16[8,80,256]{2,1,0:T(8,128)(2,1)}, f32[2,48,768]{2,1,0:T(8,128)}, f32[8,128]{1,0:T(8,128)}) custom-call(bf16[768,1024]{1,0:T(8,128)(2,1)} %get-tuple-element.36.a0t_hbm, bf16[1024,768]{1,0:T(8,128)(2,1)} %get-tuple-element.37.h_hbm, f32[1024,128]{1,0:T(8,128)} %get-tuple-element.38.scale_hbm, ...), custom_call_target="tpu_custom_call" | custom-call | flops 57982058496 | bytes 209715200 | tf_op jit(solution)/shard_map/layer0/pallas_call | solution.py:973
  287.5 5.9 %optimizer.1 = (bf16[8,80,256]{2,1,0:T(8,128)(2,1)}, bf16[2,48,768]{2,1,0:T(8,128)(2,1)}, f32[6,2,6144]{2,1,0:T(2,128)}, f32[6,2,6144]{2,1,0:T(2,128)}, f32[2,48...) custom-call(bf16[8,80,256]{2,1,0:T(8,128)(2,1)} %get-tuple-element.45.take_ref, ...), custom_call_target="tpu_custom_call" | custom-call | tf_op jit(solution)/shard_map/optimizer/pallas_call | solution.py:1045
  293.4 124.5 %all_gather.1 = (bf16[2,2,4,4,48,6144]{5,4,3,2,1,0:T(8,128)(2,1)S(1)}, bf16[4,4,4,2,48,768]{5,4,3,2,1,0:T(8,128)(2,1)S(1)}, bf16[4,4,4,2,48,512]{5,4,3,2,1,0:T(8,128)(2,1)S(1)}, bf16[4,4,4,2,48,256]{5,4,3,2,1,0:T(8,128)(2,1)}) custom-call(bf16[8,80,256]{2,1,0:T(8,128)(2,1)} %get-tuple-element.48.rows_ref, bf16[2,48,768]{2,1,0:T(8,128)(2,1)} %get-tuple-element.49.down_ref), custom_call_target="tpu_custom_call" | custom-call | tf_op jit(solution)/shard_map/all_gather/pallas_call | solution.py:521
  417.9 18.5 %put.1 = (bf16[2,4,4,48,6144]{4,3,2,1,0:T(8,128)(2,1)}, bf16[2,4,4,48,6144]{4,3,2,1,0:T(8,128)(2,1)}, bf16[2,4,4,4,2,48,768]{6,5,4,3,2,1,0:T(8,128)(2,1)}) custom-call(bf16[2,2,4,4,48,6144]{5,4,3,2,1,0:T(8,128)(2,1)S(1)} %get-tuple-element.50.wide_ref, bf16[4,4,4,2,48,768]{5,4,3,2,1,0:T(8,128)(2,1)S(1)} %get-tuple-element.51.down0_ref, ...), custom_call_target="tpu_custom_call" | custom-call | tf_op jit(solution)/shard_map/put/pallas_call | solution.py:562
